TPU v7x, 256 devices: a whole 4x4x8 slice. The times are simulated.
256 devices in a mesh: px: 8 (over z_lo, core), pz: 32 (over z_hi, y, x).
Axes of the slice: x: 4, y: 4, z: 8 (z_hi: 2, z_lo: 4; z = z_hi * 4 + z_lo), core: 2. Of those that a mesh axis runs over, the one named last changes fastest.
Arguments:
- velocity: float32 [3, 256, 64, 1024], P(None, 'pz', None, 'px'), may hold values from -8 to 8, as said below
- filter_inverse: float32 [256, 256], replicated, may hold values from 0 to 2, as said below
- filter_block: int32 [256], replicated, may hold values from 0 to 7, never falling along the last dimension, each value on 1 to 128 neighbouring positions
- plane_bin: int32 [256], replicated, may hold values from 0 to 63, never falling along the last dimension, each value on 1 to 16 neighbouring positions
Outputs:
- leonard: float32 [6, 256, 64, 1024], P(None, 'pz', None, 'px')
- viscosity: float32 [256, 64, 1024], P('pz', None, 'px')
- coefficient: float32 [256], replicated
Inputs may be any that keep to these rules, and one draw needn't show every extreme that they name: `velocity`: each component is a rough random field. `filter_inverse`: entries are positive. `filter_block`: never falls along the planes; each of the 8 blocks holds 1 to 128 consecutive planes, one exactly 128. `plane_bin`: never falls along the planes; each of the 64 bins holds 1 to 16 consecutive planes, one exactly 16.
All inputs are finite; a program needn't handle non-finite values.
Results may differ from a plain program's by a relative error of at most 0.0003.
Values sent between devices are 32-bit elements; how exact they have to be, the bound alone decides.
A program may use at most 128 MiB of HBM per device.

v0:
```python
import jax
import jax.numpy as jnp
from jax import lax
from jax.sharding import Mesh
from jax.sharding import PartitionSpec as P

NBIN = 64
PZ = ("pz_0", "pz_1", "pz_2")
PX = ("px_0", "px_1")
PX_PZ = ("px_0", "px_1", "pz_0", "pz_1", "pz_2")


def with_halo(cells, sides, width):
    for axis, dim in sides:
        count = lax.axis_size(axis)
        head = lax.slice_in_dim(cells, 0, width, axis=dim)
        tail = lax.slice_in_dim(cells, cells.shape[dim] - width, cells.shape[dim], axis=dim)
        cells = jnp.concatenate(
            [
                lax.ppermute(tail, axis, [(i, (i + 1) % count) for i in range(count)]),
                cells,
                lax.ppermute(head, axis, [((i + 1) % count, i) for i in range(count)]),
            ],
            axis=dim,
        )
    return cells


def over_axes(x, axes):
    for axis in axes:
        x = lax.psum(x, axis)
    return x


def in_blocks(x, dim, peers):
    shape = x.shape
    tiles = x.reshape(*shape[:dim], peers, shape[dim] // peers, *shape[dim + 1 :])
    return jnp.moveaxis(tiles, dim, 0)


def cut_rows(length, count):
    unit = 8 if length >= 8 * count else 1
    return [length // unit * k // count * unit for k in range(1, count)]


def laid_out(tiles, dim):
    tiles = jnp.moveaxis(tiles, 0, dim)
    shape = tiles.shape
    return tiles.reshape(*shape[:dim], shape[dim] * shape[dim + 1], *shape[dim + 2 :])


def several_exchanges(x, axis, pieces, split_dim, concat_dim):
    tiles = in_blocks(x, split_dim, lax.axis_size(axis))
    split_at = max(range(1, max(2, tiles.ndim - 1)), key=lambda d: tiles.shape[d])
    outs = []
    for share in jnp.split(tiles, cut_rows(tiles.shape[split_at], pieces), axis=split_at):
        if share.size:
            outs.append(lax.all_to_all(share, axis, split_axis=0, concat_axis=0, tiled=True))
    return laid_out(jnp.concatenate(outs, axis=split_at), concat_dim)


def quantities(padded):
    centre = padded[:, 1:-1, 1:-1, 1:-1]
    along_y = (padded[:, 2:, 1:-1, 1:-1] - padded[:, :-2, 1:-1, 1:-1]) * 0.5
    along_z = (padded[:, 1:-1, 2:, 1:-1] - padded[:, 1:-1, :-2, 1:-1]) * 0.5
    along_x = (padded[:, 1:-1, 1:-1, 2:] - padded[:, 1:-1, 1:-1, :-2]) * 0.5
    strain = jnp.stack(
        [
            along_x[0],
            along_y[1],
            along_z[2],
            0.5 * (along_y[0] + along_x[1]),
            0.5 * (along_z[0] + along_x[2]),
            0.5 * (along_z[1] + along_y[2]),
        ]
    )
    magnitude = jnp.sqrt(
        2.0 * jnp.sum(strain[:3] * strain[:3], axis=0)
        + 4.0 * jnp.sum(strain[3:] * strain[3:], axis=0)
    )
    products = jnp.stack(
        [
            centre[0] * centre[0],
            centre[1] * centre[1],
            centre[2] * centre[2],
            centre[0] * centre[1],
            centre[0] * centre[2],
            centre[1] * centre[2],
        ]
    )
    fields = jnp.concatenate([centre, strain, products, magnitude[None] * strain], axis=0)
    along = (fields[..., :-2] + 2.0 * fields[..., 1:-1] + fields[..., 2:]) * 0.25
    boxed = (along[:, :, :-2] + 2.0 * along[:, :, 1:-1] + along[:, :, 2:]) * 0.25
    return (boxed, magnitude[:, 1:-1, 1:-1])


def contract(filtered):
    speed = filtered[0:3]
    strain = filtered[3:9]
    products = filtered[9:15]
    scaled = filtered[15:21]
    leonard = products - jnp.stack(
        [
            speed[0] * speed[0],
            speed[1] * speed[1],
            speed[2] * speed[2],
            speed[0] * speed[1],
            speed[0] * speed[2],
            speed[1] * speed[2],
        ]
    )
    fmag = jnp.sqrt(
        2.0 * jnp.sum(strain[:3] * strain[:3], axis=0)
        + 4.0 * jnp.sum(strain[3:] * strain[3:], axis=0)
    )
    model = scaled - 4.0 * fmag[None] * strain
    weights = jnp.array([1.0, 1.0, 1.0, 2.0, 2.0, 2.0], jnp.float32).reshape(6, 1, 1, 1)
    product_lm = jnp.sum(weights * leonard * model, axis=0)
    product_mm = jnp.sum(weights * model * model, axis=0)
    return (leonard, product_lm, product_mm)


def local(velocity, filter_inverse, filter_block, plane_bin):
    same = (filter_block[:, None] == filter_block[None, :]).astype(jnp.float32)
    masked = filter_inverse * same
    weights = masked / jnp.sum(masked, axis=1, keepdims=True)
    columns = lax.all_to_all(velocity, PZ, split_axis=2, concat_axis=1, tiled=True)
    extended = with_halo(columns, ((PX, 3),), 2)
    extended = with_halo(extended, ((PZ, 2),), 2)
    extended = jnp.pad(extended, ((0, 0), (1, 1), (0, 0), (0, 0)))
    boxed, magnitude = quantities(extended)
    filtered = jnp.einsum("ab,kbzx->kazx", weights, boxed, precision=lax.Precision.HIGHEST)
    leonard, product_lm, product_mm = contract(filtered)
    onehot = (plane_bin[:, None] == jnp.arange(NBIN, dtype=jnp.int32)[None, :]).astype(jnp.float32)
    local_lm = jnp.dot(jnp.sum(product_lm, axis=(1, 2)), onehot, precision=lax.Precision.HIGHEST)
    local_mm = jnp.dot(jnp.sum(product_mm, axis=(1, 2)), onehot, precision=lax.Precision.HIGHEST)
    numer, denom = (over_axes(local_lm, PX_PZ), over_axes(local_mm, PX_PZ))
    cells = filtered.shape[3] * lax.axis_size(PX) * filtered.shape[2] * lax.axis_size(PZ)
    per_bin = numer / jnp.maximum(denom, jnp.float32(cells))
    coefficient = jnp.dot(onehot, per_bin, precision=lax.Precision.HIGHEST)
    column_visc = coefficient[:, None, None] * magnitude
    stacked = jnp.concatenate([leonard, column_visc[None]], axis=0)
    returned = several_exchanges(stacked, PZ, 2, 1, 2)
    leonard_back = returned[:6]
    viscosity = returned[6]
    return (leonard_back, viscosity, coefficient)


def solution(mesh):
    finer = Mesh(mesh.devices.reshape(4, 2, 2, 4, 4), ("px_0", "px_1", "pz_0", "pz_1", "pz_2"))
    return jax.shard_map(
        local,
        mesh=finer,
        in_specs=(P(None, PZ, None, PX), P(), P(), P()),
        out_specs=(P(None, PZ, None, PX), P(PZ, None, PX), P()),
        check_vma=False,
    )
```

profile of v0, /device:TPU:32, one launch (start us, length us, event | category | flops | bytes accessed | tf_op | source)
XLA Modules:
  0.0 264.0 jit_solution(12930660973001076615)
XLA Ops:
  0.6 1.6 copy.21
  2.2 39.1 %all_to_all.28 = f32[3,8,64,128]{3,1,0,2:T(8,128)S(1)} all-to-all(f32[3,8,64,128]{3,1,0,2:T(8,128)S(1)} %copy.21), channel_id=1, replica_groups=mesh['px_0'=4,'px_1'=2,'pz_0'=2,'pz_1'=4,'pz_2'=4] {'pz_0','pz_1','pz_2'}, dimensions={2} | all-to-all | bytes 1572864 | tf_op jit(solution)/shard_map/all_to_all | solution.py:127
  42.3 1.8 collective-permute-start.1
  45.8 1.8 pad_maximum_fusion.8
  47.6 2.5 copy.28
  50.1 2.6 collective-permute-start.3
  52.9 33.0 %collective-permute-done.3 = f32[3,256,2,132]{1,2,3,0:T(2,128)} collective-permute-done((f32[3,256,2,132]{1,2,3,0:T(2,128)}, f32[3,256,2,132]{1,2,3,0:T(2,128)}, u32[]{:S(2)}, u32[]{:S(2)}) %collective-permute-start.3) | collective-permute-done | bytes 811040 | tf_op jit(solution)/shard_map/ppermute | solution.py:22
  87.4 8.9 %collective-permute-done.2 = f32[3,256,2,132]{1,2,3,0:T(2,128)} collective-permute-done((f32[3,256,2,132]{1,2,3,0:T(2,128)}, f32[3,256,2,132]{1,2,3,0:T(2,128)}, u32[]{:S(2)}, u32[]{:S(2)}) %collective-permute-start.2) | collective-permute-done | bytes 811040 | tf_op jit(solution)/shard_map/ppermute | solution.py:20
  96.3 2.5 copy.30
  98.7 5.0 %fusion.11 = f32[3,256,4,130]{3,1,2,0:T(8,128)S(1)} fusion(f32[3,256,2,132]{3,1,2,0:T(8,128)} %copy.30, f32[3,256,2,2]{3,1,2,0:T(8,128)} %copy-done.1, f32[3,256,2,128]{3,1,2,0:T(8,128)S(1)} %bitcast.36, f32[3,256,2,2]{3,1,2,0:T(8,128)S(1)} %copy.26, f32[3,256,2,132]{3,1,2,0:T(8,128)S(1)} %copy.31), kind=kLoop, calls=%fused_computation.18 | loop fusion | flops 3194880 | bytes 4030464 | tf_op jit(solution)/shard_map/mul | solution.py:65
  105.1 4.6 %slice_dynamic-update-slice_fusion = (f32[21,256,4,130]{3,1,2,0:T(8,128)}, f32[3,256,4,130]{3,1,2,0:T(8,128)S(1)}, f32[3,256,4,130]{3,1,2,0:T(8,128)S(1)}) fusion(f32[3,256,6,132]{3,1,2,0:T(8,128)S(1)} %pad_maximum_fusion), kind=kLoop, calls=%fused_computation.26 | loop fusion | flops 1597439 | bytes 20496384
  121.3 1.7 multiply_dynamic-update-slice_fusion.3
  124.6 1.6 multiply_dynamic-update-slice_fusion.1
  126.9 3.1 %multiply_dynamic-update-slice_fusion = f32[21,256,4,130]{3,1,2,0:T(8,128)} fusion(f32[21,256,4,130]{3,1,2,0:T(8,128)} %multiply_dynamic-update-slice_fusion.1, f32[6,256,4,130]{3,1,2,0:T(8,128)S(1)} %get-tuple-element.24, f32[256,4,130]{2,0,1:T(8,128)S(1)} %add_sqrt_fusion), kind=kLoop, calls=%fused_computation.4 | loop fusion | flops 798720 | bytes 10018816 | tf_op jit(solution)/shard_map/concatenate | solution.py:91
  130.0 21.8 %fusion = f32[21,256,4,128]{3,1,2,0:T(8,128)S(1)} fusion(f32[21,256,4,130]{3,1,2,0:T(8,128)} %multiply_dynamic-update-slice_fusion), kind=kLoop, calls=%fused_computation.1 | loop fusion | flops 11010048 | bytes 44040192 | tf_op jit(solution)/shard_map/mul | solution.py:92
  151.8 9.6 %fusion.17 = f32[21,256,2,128]{1,3,2,0:T(8,128)S(1)} fusion(f32[21,256,4,128]{3,1,2,0:T(8,128)S(1)} %fusion, f32[256,256]{1,0:T(8,128)S(1)} %copy-done.3, f32[256]{0:T(256)S(1)} %fusion.30, s32[256]{0:T(256)S(1)} %copy-done.4), kind=kOutput, calls=%fused_computation.33 | convolution fusion | flops 4233560064 | bytes 22285312 | tf_op jit(solution)/shard_map/ab,kbzx->kazx/dot_general | solution.py:132
  163.3 10.3 %all-reduce.3 = (f32[64]{0:T(128)S(1)}, f32[64]{0:T(128)S(1)}) all-reduce(f32[64]{0:T(128)S(1)} %convolution_bitcast_fusion.1, f32[64]{0:T(128)S(1)} %convolution_bitcast_fusion), channel_id=1, replica_groups=mesh['px_0'=4,'px_1'=2,'pz_0'=2,'pz_1'=4,'pz_2'=4] {'px_0'}, use_global_device_ids=true, to_apply=%region_6.7 | all-reduce | flops 128 | bytes 1024 | tf_op jit(solution)/shard_map/psum | solution.py:31
  173.5 2.5 all-reduce.5
  176.0 8.8 %all-reduce.4 = (f32[64]{0:T(128)S(1)}, f32[64]{0:T(128)S(1)}) all-reduce(f32[64]{0:T(128)S(1)} %get-tuple-element.21, f32[64]{0:T(128)S(1)} %get-tuple-element.22), channel_id=1, replica_groups=mesh['px_0'=4,'px_1'=2,'pz_0'=2,'pz_1'=4,'pz_2'=4] {'pz_0'}, use_global_device_ids=true, to_apply=%region_8.9 | all-reduce | flops 128 | bytes 1024 | tf_op jit(solution)/shard_map/psum | solution.py:31
  184.8 7.7 %all-reduce.2 = (f32[64]{0:T(128)S(1)}, f32[64]{0:T(128)S(1)}) all-reduce(f32[64]{0:T(128)S(1)} %get-tuple-element.19, f32[64]{0:T(128)S(1)} %get-tuple-element.20), channel_id=1, replica_groups=mesh['px_0'=4,'px_1'=2,'pz_0'=2,'pz_1'=4,'pz_2'=4] {'pz_1'}, use_global_device_ids=true, to_apply=%region_9.10 | all-reduce | flops 128 | bytes 1024 | tf_op jit(solution)/shard_map/psum | solution.py:31
  192.5 9.5 %all-reduce.1 = (f32[64]{0:T(128)S(1)}, f32[64]{0:T(128)S(1)}) all-reduce(f32[64]{0:T(128)S(1)} %get-tuple-element.15, f32[64]{0:T(128)S(1)} %get-tuple-element.16), channel_id=1, replica_groups=mesh['px_0'=4,'px_1'=2,'pz_0'=2,'pz_1'=4,'pz_2'=4] {'pz_2'}, use_global_device_ids=true, to_apply=%region_10.11 | all-reduce | flops 128 | bytes 1024 | tf_op jit(solution)/shard_map/psum | solution.py:31
  204.5 7.7 %all-to-all-start.1 = ((f32[32,7,4,2,128]{4,2,3,1,0:T(4,128)}), f32[32,7,4,2,128]{4,2,3,1,0:T(4,128)S(1)}, u32[]{:S(2)}, u32[]{:S(2)}) async-start(f32[32,7,4,2,128]{4,2,3,1,0:T(4,128)} %copy.36), calls=%async_computation.1 | async-start | bytes 1835008 | tf_op jit(solution)/shard_map/all_to_all | solution.py:58
  212.4 24.1 %all-to-all-done.1 = f32[32,7,4,2,128]{4,2,3,1,0:T(4,128)S(1)} async-done(((f32[32,7,4,2,128]{4,2,3,1,0:T(4,128)}), f32[32,7,4,2,128]{4,2,3,1,0:T(4,128)S(1)}, u32[]{:S(2)}, u32[]{:S(2)}) %all-to-all-start.1) | async-done | bytes 917536 | tf_op jit(solution)/shard_map/all_to_all | solution.py:58
  236.4 24.9 %all_to_all.29 = f32[32,7,4,2,128]{4,2,3,1,0:T(4,128)S(1)} all-to-all(f32[32,7,4,2,128]{4,2,3,1,0:T(4,128)S(1)} %copy.37), channel_id=1, replica_groups=mesh['px_0'=4,'px_1'=2,'pz_0'=2,'pz_1'=4,'pz_2'=4] {'pz_0','pz_1','pz_2'}, dimensions={0} | all-to-all | bytes 1835008 | tf_op jit(solution)/shard_map/all_to_all | solution.py:58
  (67 shorter events, 26.5 us)
Async XLA Ops:
  41.7 11.0 %copy-start.3 = (f32[256,256]{1,0:T(8,128)S(1)}, f32[256,256]{1,0:T(8,128)}, u32[]{:S(2)}) copy-start(f32[256,256]{1,0:T(8,128)} %param.6) | copy-start | bytes 786436
  41.7 11.0 %copy-start.4 = (s32[256]{0:T(256)S(1)}, s32[256]{0:T(256)}, u32[]{:S(2)}) copy-start(s32[256]{0:T(256)} %param.7) | copy-start | bytes 3076
  41.9 3.2 %collective-permute-start = (f32[3,256,2,2]{1,3,2,0:T(2,128)S(1)}, f32[3,256,2,2]{1,3,2,0:T(2,128)S(1)}, u32[]{:S(2)}, u32[]{:S(2)}) collective-permute-start(f32[3,256,2,2]{1,3,2,0:T(2,128)S(1)} %copy.24), channel_id=1, source_target_pairs={{0,32},{32,64},{64,96},{96,128},{128,160},{160,192},{192,224},{224... | collective-permute-start | bytes 36872 | tf_op jit(solution)/shard_map/ppermute | solution.py:20
  42.3 3.2 %collective-permute-start.1 = (f32[3,256,2,2]{1,3,2,0:T(2,128)S(1)}, f32[3,256,2,2]{1,3,2,0:T(2,128)S(1)}, u32[]{:S(2)}, u32[]{:S(2)}) collective-permute-start(f32[3,256,2,2]{1,3,2,0:T(2,128)S(1)} %copy.25), channel_id=1, source_target_pairs={{32,0},{64,32},{96,64},{128,96},{160,128},{192,160},{224,192},{0,2... | collective-permute-start | bytes 36872 | tf_op jit(solution)/shard_map/ppermute | solution.py:22
  45.8 7.1 %copy-start.1 = (f32[3,256,2,2]{3,1,2,0:T(8,128)}, f32[3,256,2,2]{3,1,2,0:T(8,128)S(1)}, u32[]{:S(2)}) copy-start(f32[3,256,2,2]{3,1,2,0:T(8,128)S(1)} %copy.27) | copy-start | bytes 36868
  50.1 35.8 %collective-permute-start.3 = (f32[3,256,2,132]{1,2,3,0:T(2,128)}, f32[3,256,2,132]{1,2,3,0:T(2,128)}, u32[]{:S(2)}, u32[]{:S(2)}) collective-permute-start(f32[3,256,2,132]{1,2,3,0:T(2,128)} %copy.28), channel_id=1, source_target_pairs={{1,0},{2,1},{3,2},{4,3},{5,4},{6,5},{7,6},{8,7},{9,8},{10,9},{11,1... | collective-permute-start | bytes 2433032 | tf_op jit(solution)/shard_map/ppermute | solution.py:22
  52.7 43.6 %collective-permute-start.2 = (f32[3,256,2,132]{1,2,3,0:T(2,128)}, f32[3,256,2,132]{1,2,3,0:T(2,128)}, u32[]{:S(2)}, u32[]{:S(2)}) collective-permute-start(f32[3,256,2,132]{1,2,3,0:T(2,128)} %copy.28), channel_id=1, source_target_pairs={{0,1},{1,2},{2,3},{3,4},{4,5},{5,6},{6,7},{7,8},{8,9},{9,10},{10,1... | collective-permute-start | bytes 2433032 | tf_op jit(solution)/shard_map/ppermute | solution.py:20
  98.7 5.0 %copy-start = (f32[3,256,2,132]{3,1,2,0:T(8,128)S(1)}, f32[3,256,2,132]{3,1,2,0:T(8,128)}, u32[]{:S(2)}) copy-start(f32[3,256,2,132]{3,1,2,0:T(8,128)} %copy.30) | copy-start | bytes 2433028
  98.7 5.0 %copy-start.2 = (f32[3,256,2,2]{3,1,2,0:T(8,128)S(1)}, f32[3,256,2,2]{3,1,2,0:T(8,128)}, u32[]{:S(2)}) copy-start(f32[3,256,2,2]{3,1,2,0:T(8,128)} %copy-done.1) | copy-start | bytes 36868
  161.4 0.7 copy-start.6
  161.8 1.0 copy-start.7
  202.3 1.2 copy-start.5
  204.5 31.9 %all-to-all-start.1 = ((f32[32,7,4,2,128]{4,2,3,1,0:T(4,128)}), f32[32,7,4,2,128]{4,2,3,1,0:T(4,128)S(1)}, u32[]{:S(2)}, u32[]{:S(2)}) async-start(f32[32,7,4,2,128]{4,2,3,1,0:T(4,128)} %copy.36), calls=%async_computation.1 | async-start | bytes 1835008 | tf_op jit(solution)/shard_map/all_to_all | solution.py:58
where the time goes:
time: 265 us; the launch traced here: 264 us
  blocking collectives  103 us (39%)
  waiting for transfers between devices  67 us (25%)
  other arithmetic  51.1 us (19%)
  local copies, waits for them, and re-layouts  19.8 us (7%)
  starting transfers between devices  12.1 us (5%)
  matrix products  10.3 us (4%)
    all_to_all x1, blocking collectives, local(): lax.all_to_all(velocity, PZ, split_axis=2, concat_axis=1, tiled=True)  39.1 us
    psum x5, blocking collectives, over_axes(): x = lax.psum(x, axis)  38.8 us
    ppermute x2, waiting for transfers between devices, with_halo(): lax.ppermute(head, axis, [((i + 1) % count, i) for i in range(count)])  33 us
    all_to_all x1, blocking collectives, several_exchanges(): lax.all_to_all(share, axis, split_axis=0, concat_axis=0, tiled=True)  24.9 us
    all_to_all x1, waiting for transfers between devices, several_exchanges(): lax.all_to_all(share, axis, split_axis=0, concat_axis=0, tiled=True)  24.1 us
    mul x1, other arithmetic, quantities(): (fields[..., :-2] + 2.0 * fields[..., 1:-1] + fields[..., 2:]) * 0.25  21.8 us
    unnamed x14, other arithmetic  14.9 us
    ppermute x2, waiting for transfers between devices, with_halo(): lax.ppermute(tail, axis, [(i, (i + 1) % count) for i in range(count)])  9.92 us
  transfers between devices with their start and end apart: 5, of which 4 were waited for; matrix products, arithmetic and copies ran while one was open for 1% of the time, Pallas kernels for 0%

commit v1 on v0

v1 whole, which is shorter than its diff:
```python
import functools

import jax
import jax.numpy as jnp
from jax import lax
from jax.experimental import pallas as pl
from jax.experimental.pallas import tpu as pltpu
from jax.sharding import PartitionSpec as P

NBIN = 64
MESH = pl.DeviceIdType.MESH
F32 = jnp.float32
BF16 = jnp.bfloat16
VMEM = pltpu.VMEM
UNITS = 9
READY = (3, 6, 8, 9)


def to_columns(vel_ref, x_ref, mix):
    even = lax.broadcasted_iota(jnp.int32, (64, 128), 1) % 2 == 0

    def plane(y, _):
        for f in range(3):
            v = vel_ref[f, y]
            mix[f, pl.ds(0, 64, stride=2), :] = v
            mix[f, pl.ds(1, 64, stride=2), :] = v
            t = mix[f].T
            x_ref[pl.ds(f * 8 + y, 64, stride=24), :] = jnp.where(even, t[:64], t[64:])
        return 0

    lax.fori_loop(0, 8, plane, 0)


def where_am_i():
    px, pz = lax.axis_index("px"), lax.axis_index("pz")
    return px, pz, pz // 16, (pz % 16) // 4, pz % 4


def spread(x_ref, r_ref, partner, send_a, recv_a, send_b, recv_b, send_c, recv_c, local):
    px, pz, h, yy, xx = where_am_i()
    i = pz % 16
    other = 1 - h
    barrier = pltpu.get_barrier_semaphore()
    pl.semaphore_signal(barrier, inc=1, device_id=(px, other * 16 + i), device_id_type=MESH)
    for k in range(1, 16):
        j = ((yy + k // 4) % 4) * 4 + (xx + k % 4) % 4
        pl.semaphore_signal(barrier, inc=1, device_id=(px, h * 16 + j), device_id_type=MESH)
    pl.semaphore_wait(barrier, 16)

    def unit(n):
        u = (2 * yy + n) % UNITS
        return pltpu.make_async_remote_copy(
            src_ref=x_ref.at[pl.ds(other * 32 + u * 4, 4)],
            dst_ref=partner.at[pl.ds(u * 4, 4)],
            send_sem=send_a.at[n],
            recv_sem=recv_a.at[n],
            device_id=(px, other * 16 + i),
            device_id_type=MESH,
        )

    def own(k):
        j = ((yy + k // 4) % 4) * 4 + (xx + k % 4) % 4
        return pltpu.make_async_remote_copy(
            src_ref=x_ref.at[pl.ds((h * 16 + j) * 2, 6)],
            dst_ref=r_ref.at[:, :, pl.ds(pl.multiple_of(pz * 8, 8), 8), :],
            send_sem=send_b.at[k],
            recv_sem=recv_b.at[k],
            device_id=(px, h * 16 + j),
            device_id_type=MESH,
        )

    def theirs(k):
        j = ((yy + k // 4) % 4) * 4 + (xx + k % 4) % 4
        return pltpu.make_async_remote_copy(
            src_ref=partner.at[pl.ds(j * 2, 6)],
            dst_ref=r_ref.at[:, :, pl.ds(pl.multiple_of((other * 16 + i) * 8, 8), 8), :],
            send_sem=send_c.at[k],
            recv_sem=recv_c.at[k],
            device_id=(px, h * 16 + j),
            device_id_type=MESH,
        )

    for n in range(UNITS):
        unit(n).start()
    for k in range(1, 16):
        own(k).start()
    here = pltpu.make_async_copy(
        x_ref.at[pl.ds(pz * 2, 6)],
        r_ref.at[:, :, pl.ds(pl.multiple_of(pz * 8, 8), 8), :],
        local.at[0],
    )
    here.start()
    there = pltpu.make_async_copy(
        partner.at[pl.ds(i * 2, 6)],
        r_ref.at[:, :, pl.ds(pl.multiple_of((other * 16 + i) * 8, 8), 8), :],
        local.at[1],
    )
    done = 0
    for row in range(4):
        while done < READY[row]:
            unit(done).wait_recv()
            done += 1
        for col in range(4):
            k = row * 4 + col
            if k == 0:
                there.start()
            else:
                theirs(k).start()
    here.wait()
    there.wait()
    for n in range(UNITS):
        unit(n).wait_send()
    for k in range(1, 16):
        own(k).wait()
        theirs(k).wait()


def fields_of(u, gx, up, down):
    def d_x(f):
        return (u[f][gx + 1] - u[f][gx - 1]) * 0.5

    def d_z(f):
        return (pltpu.roll(u[f][gx], 126, 1) - pltpu.roll(u[f][gx], 2, 1)) * 0.5

    def d_y(f):
        return (up[f] - down[f]) * 0.5

    s = [
        d_x(0),
        d_y(1),
        d_z(2),
        0.5 * (d_y(0) + d_x(1)),
        0.5 * (d_z(0) + d_x(2)),
        0.5 * (d_z(1) + d_y(2)),
    ]
    mag = jnp.sqrt(
        2.0 * (s[0] * s[0] + s[1] * s[1] + s[2] * s[2])
        + 4.0 * (s[3] * s[3] + s[4] * s[4] + s[5] * s[5])
    )
    a, b, c = u[0][gx], u[1][gx], u[2][gx]
    return [a, b, c] + s + [a * a, b * b, c * c, a * b, a * c, b * c] + [mag * t for t in s], mag


def math(r_ref, inv_ref, fbc_ref, fbr_ref, pbc_ref, l_ref, part_ref, g, bh, bl, ff, wh, wl):
    masked = jnp.where(fbc_ref[...] == fbr_ref[...], inv_ref[...], 0.0)
    w = masked / jnp.sum(masked, axis=1, keepdims=True)
    w_hi = w.astype(BF16)
    wh[...] = w_hi
    wl[...] = (w - w_hi.astype(F32)).astype(BF16)

    def strip(c, _):
        y0 = pl.multiple_of(c * 16, 16)
        before = pl.multiple_of(jnp.maximum(y0 - 8, 0), 8)
        after = pl.multiple_of(jnp.minimum(y0 + 16, 248), 8)
        first, last = c == 0, c == 15
        u = [[r_ref[x, f, pl.ds(y0, 16), :] for x in range(6)] for f in range(3)]
        for gx in range(1, 5):
            up, down = [], []
            for f in range(3):
                prev = jnp.where(first, 0.0, r_ref[gx, f, pl.ds(before, 8), :])
                succ = jnp.where(last, 0.0, r_ref[gx, f, pl.ds(after, 8), :])
                down.append(jnp.concatenate([prev[7:], u[f][gx][:15]], axis=0))
                up.append(jnp.concatenate([u[f][gx][1:], succ[:1]], axis=0))
            out, mag = fields_of(u, gx, up, down)
            for k in range(21):
                g[k, gx - 1] = out[k]
            if gx in (2, 3):
                l_ref[2 * c, gx - 2, 6] = mag[:8]
                l_ref[2 * c + 1, gx - 2, 6] = mag[8:]
        for k in range(21):
            g1, g2 = g[k, 1], g[k, 2]
            for x, total in ((0, g[k, 0] + 2.0 * g1 + g2), (1, g1 + 2.0 * g2 + g[k, 3])):
                box = (pltpu.roll(total, 2, 1) + 2.0 * total + pltpu.roll(total, 126, 1)) * 0.0625
                hi = box.astype(BF16)
                bh[k, pl.ds(y0, 16), pl.ds(x * 128, 128)] = hi
                bl[k, pl.ds(y0, 16), pl.ds(x * 128, 128)] = (box - hi.astype(F32)).astype(BF16)
        return 0

    lax.fori_loop(0, 16, strip, 0)

    def product(k, _):
        hi, lo = bh[k], bl[k]
        acc = jnp.dot(wh[...], lo, preferred_element_type=F32)
        acc += jnp.dot(wl[...], hi, preferred_element_type=F32)
        ff[k] = acc + jnp.dot(wh[...], hi, preferred_element_type=F32)
        return 0

    lax.fori_loop(0, 21, product, 0)

    lanes = lax.broadcasted_iota(jnp.int32, (8, 128), 1)

    def contract(c, sums):
        y0 = pl.multiple_of(c * 8, 8)
        lm_sum, mm_sum = 0.0, 0.0
        for x in range(2):
            f = [ff[k, pl.ds(y0, 8), pl.ds(x * 128, 128)] for k in range(21)]
            a, b, d = f[0], f[1], f[2]
            s, p, m = f[3:9], f[9:15], f[15:21]
            uu = [a * a, b * b, d * d, a * b, a * d, b * d]
            fmag = jnp.sqrt(
                2.0 * (s[0] * s[0] + s[1] * s[1] + s[2] * s[2])
                + 4.0 * (s[3] * s[3] + s[4] * s[4] + s[5] * s[5])
            )
            lm, mm = [], []
            for k in range(6):
                leo = p[k] - uu[k]
                l_ref[c, x, k] = leo
                mod = m[k] - 4.0 * fmag * s[k]
                lm.append(leo * mod)
                mm.append(mod * mod)
            lm_sum += lm[0] + lm[1] + lm[2] + 2.0 * (lm[3] + lm[4] + lm[5])
            mm_sum += mm[0] + mm[1] + mm[2] + 2.0 * (mm[3] + mm[4] + mm[5])
        hot = pbc_ref[pl.ds(y0, 8), :] == lanes
        num = sums[0] + jnp.where(hot, jnp.sum(lm_sum, axis=1, keepdims=True), 0.0)
        den = sums[1] + jnp.where(hot, jnp.sum(mm_sum, axis=1, keepdims=True), 0.0)
        return num, den

    zero = jnp.zeros((8, 128), F32)
    num, den = lax.fori_loop(0, 32, contract, (zero, zero))
    row = lax.broadcasted_iota(jnp.int32, (8, 128), 0)
    num = jnp.sum(num, axis=0, keepdims=True)
    den = jnp.sum(den, axis=0, keepdims=True)
    part_ref[...] = jnp.where(row == 0, num, jnp.where(row == 1, den, 0.0))


def give_back(l_ref, part_ref, o_ref, tot_ref, a1, a2, s1, ss1, rs1, ss2, rs2, sb, rb, local):
    px, pz, h, yy, xx = where_am_i()

    def peer(k):
        return ((h + k // 16) % 2) * 16 + ((yy + (k % 16) // 4) % 4) * 4 + (xx + k % 4) % 4

    barrier = pltpu.get_barrier_semaphore()
    for k in range(1, 32):
        pl.semaphore_signal(barrier, inc=1, device_id=(px, peer(k)), device_id_type=MESH)
    for k in range(1, 8):
        pl.semaphore_signal(barrier, inc=1, device_id=((px + k) % 8, pz), device_id_type=MESH)
    pl.semaphore_wait(barrier, 38)

    def small(k):
        return pltpu.make_async_remote_copy(
            src_ref=part_ref,
            dst_ref=a1.at[pz],
            send_sem=ss1.at[k],
            recv_sem=rs1.at[k],
            device_id=(px, peer(k)),
            device_id_type=MESH,
        )

    def second(k):
        return pltpu.make_async_remote_copy(
            src_ref=s1,
            dst_ref=a2.at[px],
            send_sem=ss2.at[k],
            recv_sem=rs2.at[k],
            device_id=((px + k) % 8, pz),
            device_id_type=MESH,
        )

    def big(k):
        return pltpu.make_async_remote_copy(
            src_ref=l_ref.at[peer(k)],
            dst_ref=o_ref.at[pz],
            send_sem=sb.at[k],
            recv_sem=rb.at[k],
            device_id=(px, peer(k)),
            device_id_type=MESH,
        )

    for k in range(1, 32):
        small(k).start()
    for k in range(1, 16):
        big(k).start()
    a1[pz] = part_ref[...]
    for k in range(1, 32):
        small(k).wait_recv()
    total = a1[0]
    for q in range(1, 32):
        total = total + a1[q]
    s1[...] = total
    a2[px] = total
    here = pltpu.make_async_copy(l_ref.at[pz], o_ref.at[pz], local.at[0])
    here.start()
    for k in range(1, 8):
        second(k).start()
    for k in range(16, 32):
        big(k).start()
    for k in range(1, 8):
        second(k).wait_recv()
    total = a2[0]
    for q in range(1, 8):
        total = total + a2[q]
    tot_ref[...] = total
    here.wait()
    for k in range(1, 32):
        small(k).wait_send()
    for k in range(1, 8):
        second(k).wait_send()
    for k in range(1, 32):
        big(k).wait()


def to_planes(coef_ref, o_ref, leo_ref, visc_ref, mix):
    low = lax.broadcasted_iota(jnp.int32, (64, 128), 1) < 64

    def plane(y, _):
        for f in range(7):
            m = o_ref[pl.ds(f * 8 + y, 64, stride=56), :]
            mix[f] = jnp.concatenate([m, m], axis=0).T
            v = jnp.where(low, mix[f, pl.ds(0, 64, stride=2), :], mix[f, pl.ds(1, 64, stride=2), :])
            if f < 6:
                leo_ref[f, y] = v
            else:
                visc_ref[y] = coef_ref[y] * v
        return 0

    lax.fori_loop(0, 8, plane, 0)


def spec(space):
    return pl.BlockSpec(memory_space=space)


def params(**kw):
    return pltpu.CompilerParams(vmem_limit_bytes=56 * 1024 * 1024, **kw)


DMA = pltpu.SemaphoreType.DMA


def local_step(velocity, filter_inverse, filter_block, plane_bin):
    pz = lax.axis_index("pz")
    rows = pl.pallas_call(
        to_columns,
        out_shape=jax.ShapeDtypeStruct((64 * 24, 128), F32),
        in_specs=[spec(VMEM)],
        out_specs=spec(VMEM),
        scratch_shapes=[VMEM((3, 128, 128), F32)],
        compiler_params=params(),
        name="to_columns",
    )(velocity).reshape(64, 3, 8, 128)
    head, tail = rows[:2], rows[62:]
    left = lax.ppermute(tail, "px", [(i, (i + 1) % 8) for i in range(8)])
    right = lax.ppermute(head, "px", [((i + 1) % 8, i) for i in range(8)])
    even = lax.broadcasted_iota(jnp.int32, (2, 3, 8, 128), 3) % 2 == 0
    below = jnp.where(even, jnp.roll(left, -1, axis=3), jnp.roll(tail, 1, axis=3))
    above = jnp.where(even, jnp.roll(head, -1, axis=3), jnp.roll(right, 1, axis=3))
    rows = jnp.concatenate([below, rows, above], axis=0)
    columns = pl.pallas_call(
        spread,
        out_shape=jax.ShapeDtypeStruct((6, 3, 256, 128), F32),
        in_specs=[spec(VMEM)],
        out_specs=spec(pl.ANY),
        scratch_shapes=[
            VMEM((36, 3, 8, 128), F32),
            DMA((UNITS,)),
            DMA((UNITS,)),
            DMA((16,)),
            DMA((16,)),
            DMA((16,)),
            DMA((16,)),
            DMA((2,)),
        ],
        compiler_params=params(collective_id=0, has_side_effects=True),
        name="spread",
    )(rows)
    leo, part = pl.pallas_call(
        math,
        out_shape=(
            jax.ShapeDtypeStruct((32, 2, 7, 8, 128), F32),
            jax.ShapeDtypeStruct((8, 128), F32),
        ),
        in_specs=[spec(VMEM)] * 5,
        out_specs=(spec(VMEM), spec(VMEM)),
        scratch_shapes=[
            VMEM((21, 4, 16, 128), F32),
            VMEM((21, 256, 256), BF16),
            VMEM((21, 256, 256), BF16),
            VMEM((21, 256, 256), F32),
            VMEM((256, 256), BF16),
            VMEM((256, 256), BF16),
        ],
        compiler_params=params(),
        name="math",
    )(
        columns,
        filter_inverse,
        filter_block.reshape(256, 1),
        filter_block.reshape(1, 256),
        plane_bin.reshape(256, 1),
    )
    back, total = pl.pallas_call(
        give_back,
        out_shape=(
            jax.ShapeDtypeStruct((32, 2, 7, 8, 128), F32),
            jax.ShapeDtypeStruct((8, 128), F32),
        ),
        in_specs=[spec(VMEM)] * 2,
        out_specs=(spec(pl.ANY), spec(VMEM)),
        scratch_shapes=[
            VMEM((32, 8, 128), F32),
            VMEM((8, 8, 128), F32),
            VMEM((8, 128), F32),
            DMA((32,)),
            DMA((32,)),
            DMA((8,)),
            DMA((8,)),
            DMA((32,)),
            DMA((32,)),
            DMA((1,)),
        ],
        compiler_params=params(collective_id=1, has_side_effects=True),
        name="give_back",
    )(leo, part)
    per_bin = total[0, :NBIN] / jnp.maximum(total[1, :NBIN], jnp.float32(65536))
    hot = plane_bin[:, None] == jnp.arange(NBIN, dtype=jnp.int32)[None, :]
    coefficient = jnp.sum(jnp.where(hot, per_bin[None, :], 0.0), axis=1)
    mine = lax.dynamic_slice(coefficient, (pz * 8,), (8,))
    leonard, viscosity = pl.pallas_call(
        to_planes,
        out_shape=(
            jax.ShapeDtypeStruct((6, 8, 64, 128), F32),
            jax.ShapeDtypeStruct((8, 64, 128), F32),
        ),
        in_specs=[spec(pltpu.SMEM), spec(VMEM)],
        out_specs=(spec(VMEM), spec(VMEM)),
        scratch_shapes=[VMEM((7, 128, 128), F32)],
        compiler_params=params(),
        name="to_planes",
    )(mine, back.reshape(32 * 2 * 56, 128))
    return leonard, viscosity, coefficient


def solution(mesh):
    return jax.shard_map(
        local_step,
        mesh=mesh,
        in_specs=(P(None, "pz", None, "px"), P(), P(), P()),
        out_specs=(P(None, "pz", None, "px"), P("pz", None, "px"), P()),
        check_vma=False,
    )
```

time: 265 us -> 142 us (0.54)
  the two profiles are of different devices: /device:TPU:32 before, /device:TPU:104 now
where the time goes in v1:
time: 142 us; the launch traced here: 141 us
  Pallas kernels  132 us (93%)
  local copies, waits for them, and re-layouts  3.99 us (3%)
  other arithmetic  3.04 us (2%)
  starting transfers between devices  1.75 us (1%)
    pallas_call x1, Pallas kernels, local_step(): pl.pallas_call(give_back, out_shape=(jax.ShapeDtypeStruct((32, 2, 7, 8, 1...  61 us
    pallas_call x1, Pallas kernels, local_step(): pl.pallas_call(spread, out_shape=jax.ShapeDtypeStruct((6, 3, 256, 128), F...  45.1 us
    pallas_call x1, Pallas kernels, local_step(): pl.pallas_call(math, out_shape=(jax.ShapeDtypeStruct((32, 2, 7, 8, 128),...  17.7 us
    pallas_call x1, Pallas kernels, local_step(): pl.pallas_call(to_planes, out_shape=(jax.ShapeDtypeStruct((6, 8, 64, 128)...  4.77 us
    pallas_call x1, Pallas kernels, local_step(): pl.pallas_call(to_columns, out_shape=jax.ShapeDtypeStruct((64 * 24, 128),...  3.21 us
  transfers between devices with their start and end apart: 2, of which 0 were waited for; matrix products, arithmetic and copies ran while one was open for 2% of the time, Pallas kernels for 0%

profile of v1, /device:TPU:104, one launch (start us, length us, event | category | flops | bytes accessed | tf_op | source)
XLA Modules:
  0.0 141.3 jit_solution(6378421287351862841)
XLA Ops:
  0.6 0.0 copy-start
  0.6 3.2 %to_columns.1 = f32[1536,128]{1,0:T(8,128)} custom-call(f32[3,8,64,128]{3,2,1,0:T(8,128)} %vel_ref.1), custom_call_target="tpu_custom_call" | custom-call | tf_op jit(solution)/shard_map/to_columns/pallas_call | solution.py:332
  3.9 0.8 fusion.1
  4.6 0.0 collective-permute-start
  4.6 1.7 %collective-permute-start.1 = (f32[2,3,8,128]{3,2,1,0:T(8,128)S(1)}, f32[2,3,8,128]{3,2,1,0:T(8,128)S(1)}, u32[]{:S(2)}, u32[]{:S(2)}) collective-permute-start(f32[2,3,8,128]{3,2,1,0:T(8,128)S(1)} %bitcast.18), channel_id=1, source_target_pairs={{32,0},{64,32},{96,64},{128,96},{160,128},{192,160},{224,192},{0,2... | collective-permute-start | bytes 73736 | tf_op jit(solution)/shard_map/ppermute | solution.py:343
  6.4 0.1 slice.63
  6.4 0.1 slice.66
  6.5 1.5 %copy.10.pbc_ref = s32[256,1]{1,0:T(8,128)} copy(s32[256,1]{0,1:T(1,128)} %bitcast.25) | data formatting | bytes 2048 | tf_op jit(solution)/shard_map/broadcast_in_dim | solution.py:415
  8.0 0.0 copy-done
  8.0 0.8 copy.9.fbc_ref
  8.8 0.0 collective-permute-done
  8.8 0.1 slice.61
  8.9 0.0 collective-permute-done.1
  8.9 0.1 slice.68
  8.9 0.1 maximum_select_fusion
  9.0 2.1 %pad_maximum_fusion.x_ref = f32[68,3,8,128]{3,2,1,0:T(8,128)} fusion(f32[2,3,8,128]{3,2,1,0:T(8,128)S(1)} %get-tuple-element.18, f32[64,3,8,128]{3,2,1,0:T(8,128)} %bitcast.13, f32[2,3,8,128]{3,2,1,0:T(8,128)S(1)} %get-tuple-element.17), kind=kLoop, calls=%fused_computation | loop fusion | flops 417792 | bytes 1671168 | tf_op jit(solution)/shard_map/concatenate | solution.py:347
  11.1 45.1 %spread.1.r_ref = f32[6,3,256,128]{3,2,1,0:T(8,128)} custom-call(f32[68,3,8,128]{3,2,1,0:T(8,128)} %pad_maximum_fusion.x_ref), custom_call_target="tpu_custom_call" | custom-call | tf_op jit(solution)/shard_map/spread/pallas_call | solution.py:348
  56.2 0.0 copy-start.1
  56.3 17.7 %math.1 = (f32[32,2,7,8,128]{4,3,2,1,0:T(8,128)}, f32[8,128]{1,0:T(8,128)}) custom-call(f32[6,3,256,128]{3,2,1,0:T(8,128)} %spread.1.r_ref, f32[256,256]{1,0:T(8,128)} %inv_ref.1, s32[256,1]{1,0:T(8,128)} %copy.9.fbc_ref, s32[1,256]{1,0:T(1,128)} %bitcast.23, s32[256,1]{1,0:T(8,128)} %copy.10.pbc_ref), custom_call_target="tpu_custom_call" | custom-call | tf_op jit(solution)/shard_map/math/pallas_call | solution.py:366
  74.0 61.0 %give_back.1 = (f32[32,2,7,8,128]{4,3,2,1,0:T(8,128)}, f32[8,128]{1,0:T(8,128)}) custom-call(f32[32,2,7,8,128]{4,3,2,1,0:T(8,128)} %get-tuple-element.9.l_ref, f32[8,128]{1,0:T(8,128)} %get-tuple-element.10.part_ref), custom_call_target="tpu_custom_call" | custom-call | tf_op jit(solution)/shard_map/give_back/pallas_call | solution.py:391
  135.0 0.8 fusion
  135.7 0.1 select_reduce_fusion
  135.8 0.7 dynamic_slice.3.coef_ref
  136.5 4.8 %to_planes.1 = (f32[6,8,64,128]{3,2,1,0:T(8,128)}, f32[8,64,128]{2,1,0:T(8,128)}) custom-call(f32[8]{0:T(128)} %dynamic_slice.3.coef_ref, f32[3584,128]{1,0:T(8,128)} %bitcast.14), custom_call_target="tpu_custom_call" | custom-call | tf_op jit(solution)/shard_map/to_planes/pallas_call | solution.py:418
  (5 shorter events, 0.0 us)
Async XLA Ops:
  0.6 7.4 %copy-start = (s32[256]{0:T(256)S(1)}, s32[256]{0:T(256)}, u32[]{:S(2)}) copy-start(s32[256]{0:T(256)} %param.6) | copy-start | bytes 3076
  4.6 4.2 %collective-permute-start = (f32[2,3,8,128]{3,2,1,0:T(8,128)S(1)}, f32[2,3,8,128]{3,2,1,0:T(8,128)S(1)}, u32[]{:S(2)}, u32[]{:S(2)}) collective-permute-start(f32[2,3,8,128]{3,2,1,0:T(8,128)S(1)} %bitcast.15), channel_id=1, source_target_pairs={{0,32},{32,64},{64,96},{96,128},{128,160},{160,192},{192,224},{224... | collective-permute-start | bytes 73736 | tf_op jit(solution)/shard_map/ppermute | solution.py:342
  4.6 4.3 %collective-permute-start.1 = (f32[2,3,8,128]{3,2,1,0:T(8,128)S(1)}, f32[2,3,8,128]{3,2,1,0:T(8,128)S(1)}, u32[]{:S(2)}, u32[]{:S(2)}) collective-permute-start(f32[2,3,8,128]{3,2,1,0:T(8,128)S(1)} %bitcast.18), channel_id=1, source_target_pairs={{32,0},{64,32},{96,64},{128,96},{160,128},{192,160},{224,192},{0,2... | collective-permute-start | bytes 73736 | tf_op jit(solution)/shard_map/ppermute | solution.py:343
  56.2 79.5 %copy-start.1 = (s32[256]{0:T(256)S(1)}, s32[256]{0:T(256)}, u32[]{:S(2)}) copy-start(s32[256]{0:T(256)} %param.7) | copy-start | bytes 3076
  135.8 5.4 %copy-start.2 = (f32[256]{0:T(256)}, f32[256]{0:T(256)S(1)}, u32[]{:S(2)}) copy-start(f32[256]{0:T(256)S(1)} %select_reduce_fusion) | copy-start | bytes 3076

commit v2 on v1

v2 whole, which is shorter than its diff:
```python
import functools

import jax
import jax.numpy as jnp
from jax import lax
from jax.experimental import pallas as pl
from jax.experimental.pallas import tpu as pltpu
from jax.sharding import PartitionSpec as P

NBIN = 64
MESH = pl.DeviceIdType.MESH
F32 = jnp.float32
BF16 = jnp.bfloat16
VMEM = pltpu.VMEM
def to_columns(vel_ref, x_ref, right_ref, left_ref, mix):
    even = lax.broadcasted_iota(jnp.int32, (64, 128), 1) % 2 == 0

    def plane(y, _):
        for f in range(3):
            v = vel_ref[f, y]
            mix[f, pl.ds(0, 64, stride=2), :] = v
            mix[f, pl.ds(1, 64, stride=2), :] = v
            t = mix[f].T
            x_ref[pl.ds(48 + f * 8 + y, 64, stride=24), :] = jnp.where(even, t[:64], t[64:])
        return 0

    lax.fori_loop(0, 8, plane, 0)
    first, last = x_ref[48:96, :], x_ref[64 * 24 : 66 * 24, :]
    x_ref[0:48, :] = pltpu.roll(last, 1, 1)
    x_ref[66 * 24 : 68 * 24, :] = pltpu.roll(first, 127, 1)
    right_ref[...] = pltpu.roll(last, 127, 1)
    left_ref[...] = pltpu.roll(first, 1, 1)


def where_am_i():
    px, pz = lax.axis_index("px"), lax.axis_index("pz")
    return px, pz, pz // 16, (pz % 16) // 4, pz % 4


def spread(x_ref, below_ref, above_ref, r_ref, rows, partner, send_a, recv_a, send_b, recv_b, send_c, recv_c, local):
    px, pz, h, yy, xx = where_am_i()
    i = pz % 16
    other = 1 - h
    fetch = pltpu.make_async_copy(x_ref, rows, local.at[0])
    fetch.start()
    barrier = pltpu.get_barrier_semaphore()
    pl.semaphore_signal(barrier, inc=1, device_id=(px, other * 16 + i), device_id_type=MESH)
    for k in range(1, 16):
        j = ((yy + k // 4) % 4) * 4 + (xx + k % 4) % 4
        pl.semaphore_signal(barrier, inc=1, device_id=(px, h * 16 + j), device_id_type=MESH)
    fetch.wait()
    even = lax.broadcasted_iota(jnp.int32, (2, 3, 8, 128), 3) % 2 == 0
    rows[0:2] = jnp.where(even, below_ref[...], rows[0:2])
    rows[66:68] = jnp.where(even, rows[66:68], above_ref[...])
    pl.semaphore_wait(barrier, 16)

    def across(f):
        return pltpu.make_async_remote_copy(
            src_ref=rows.at[:, f],
            dst_ref=partner.at[:, f],
            send_sem=send_a.at[f],
            recv_sem=recv_a.at[f],
            device_id=(px, other * 16 + i),
            device_id_type=MESH,
        )

    def own(k):
        j = ((yy + k // 4) % 4) * 4 + (xx + k % 4) % 4
        return pltpu.make_async_remote_copy(
            src_ref=rows.at[pl.ds(j * 4, 8)],
            dst_ref=r_ref.at[:, :, pl.ds(pl.multiple_of(pz * 8, 8), 8), :],
            send_sem=send_b.at[k],
            recv_sem=recv_b.at[k],
            device_id=(px, h * 16 + j),
            device_id_type=MESH,
        )

    def theirs(f, k):
        j = ((yy + k // 4) % 4) * 4 + (xx + k % 4) % 4
        return pltpu.make_async_remote_copy(
            src_ref=partner.at[pl.ds(j * 4, 8), f],
            dst_ref=r_ref.at[:, f, pl.ds(pl.multiple_of((other * 16 + i) * 8, 8), 8), :],
            send_sem=send_c.at[f, k],
            recv_sem=recv_c.at[f, k],
            device_id=(px, h * 16 + j),
            device_id_type=MESH,
        )

    def there(f):
        return pltpu.make_async_copy(
            partner.at[pl.ds(i * 4, 8), f],
            r_ref.at[:, f, pl.ds(pl.multiple_of((other * 16 + i) * 8, 8), 8), :],
            local.at[1 + f],
        )

    for f in range(3):
        across(f).start()
    for k in range(1, 16):
        own(k).start()
    here = pltpu.make_async_copy(
        rows.at[pl.ds(i * 4, 8)],
        r_ref.at[:, :, pl.ds(pl.multiple_of(pz * 8, 8), 8), :],
        local.at[0],
    )
    here.start()
    for f in range(3):
        across(f).wait_recv()
        for k in range(1, 16):
            theirs(f, k).start()
        there(f).start()
    here.wait()
    for f in range(3):
        across(f).wait_send()
        there(f).wait()
        for k in range(1, 16):
            theirs(f, k).wait()
    for k in range(1, 16):
        own(k).wait()


def fields_of(u, gx, up, down):
    def d_x(f):
        return (u[f][gx + 1] - u[f][gx - 1]) * 0.5

    def d_z(f):
        return (pltpu.roll(u[f][gx], 126, 1) - pltpu.roll(u[f][gx], 2, 1)) * 0.5

    def d_y(f):
        return (up[f] - down[f]) * 0.5

    s = [
        d_x(0),
        d_y(1),
        d_z(2),
        0.5 * (d_y(0) + d_x(1)),
        0.5 * (d_z(0) + d_x(2)),
        0.5 * (d_z(1) + d_y(2)),
    ]
    mag = jnp.sqrt(
        2.0 * (s[0] * s[0] + s[1] * s[1] + s[2] * s[2])
        + 4.0 * (s[3] * s[3] + s[4] * s[4] + s[5] * s[5])
    )
    a, b, c = u[0][gx], u[1][gx], u[2][gx]
    return [a, b, c] + s + [a * a, b * b, c * c, a * b, a * c, b * c] + [mag * t for t in s], mag


def column(row):
    return jnp.broadcast_to(row, (128, 256)).T


def math(r_ref, inv_ref, fb_ref, pb_ref, l_ref, part_ref, g, bh, bl, ff, wh, wl, bins):
    h = lax.axis_index("pz") // 16
    r0 = pl.multiple_of(h * 128, 128)
    bins[0] = column(fb_ref[...])
    bins[1] = column(pb_ref[...])
    mine = bins[0, pl.ds(r0, 128), :]
    masked = jnp.where(jnp.concatenate([mine, mine], axis=1) == fb_ref[...], inv_ref[pl.ds(r0, 128), :], 0.0)
    w = masked / jnp.sum(masked, axis=1, keepdims=True)
    w_hi = w.astype(BF16)
    wh[...] = w_hi
    wl[...] = (w - w_hi.astype(F32)).astype(BF16)

    def strip(c, _):
        y0 = pl.multiple_of(c * 16, 16)
        before = pl.multiple_of(jnp.maximum(y0 - 8, 0), 8)
        after = pl.multiple_of(jnp.minimum(y0 + 16, 248), 8)
        first, last = c == 0, c == 15
        block = jnp.clip(2 * c - 16 * h, 0, 14)
        u = [[r_ref[x, f, pl.ds(y0, 16), :] for x in range(8)] for f in range(3)]
        for gx in range(1, 7):
            up, down = [], []
            for f in range(3):
                prev = jnp.where(first, 0.0, r_ref[gx, f, pl.ds(before, 8), :])
                succ = jnp.where(last, 0.0, r_ref[gx, f, pl.ds(after, 8), :])
                down.append(jnp.concatenate([prev[7:], u[f][gx][:15]], axis=0))
                up.append(jnp.concatenate([u[f][gx][1:], succ[:1]], axis=0))
            out, mag = fields_of(u, gx, up, down)
            for k in range(21):
                g[k, gx - 1] = out[k]
            if 2 <= gx <= 5:

                @pl.when(c // 8 == h)
                def _(mag=mag, gx=gx):
                    l_ref[block, gx - 2, 6] = mag[:8]
                    l_ref[block + 1, gx - 2, 6] = mag[8:]

        for k in range(21):
            gs = [g[k, t] for t in range(6)]
            for x in range(4):
                total = gs[x] + 2.0 * gs[x + 1] + gs[x + 2]
                box = (pltpu.roll(total, 2, 1) + 2.0 * total + pltpu.roll(total, 126, 1)) * 0.0625
                hi = box.astype(BF16)
                bh[k, pl.ds(y0, 16), pl.ds(x * 128, 128)] = hi
                bl[k, pl.ds(y0, 16), pl.ds(x * 128, 128)] = (box - hi.astype(F32)).astype(BF16)
        return 0

    lax.fori_loop(0, 16, strip, 0)

    def product(k, _):
        hi, lo = bh[k], bl[k]
        acc = jnp.dot(wh[...], lo, preferred_element_type=F32)
        acc += jnp.dot(wl[...], hi, preferred_element_type=F32)
        ff[k] = acc + jnp.dot(wh[...], hi, preferred_element_type=F32)
        return 0

    lax.fori_loop(0, 21, product, 0)

    lanes = lax.broadcasted_iota(jnp.int32, (8, 128), 1)

    def contract(c, sums):
        y0 = pl.multiple_of(c * 8, 8)
        lm_sum, mm_sum = 0.0, 0.0
        for x in range(4):
            f = [ff[k, pl.ds(y0, 8), pl.ds(x * 128, 128)] for k in range(21)]
            a, b, d = f[0], f[1], f[2]
            s, p, m = f[3:9], f[9:15], f[15:21]
            uu = [a * a, b * b, d * d, a * b, a * d, b * d]
            fmag = jnp.sqrt(
                2.0 * (s[0] * s[0] + s[1] * s[1] + s[2] * s[2])
                + 4.0 * (s[3] * s[3] + s[4] * s[4] + s[5] * s[5])
            )
            lm, mm = [], []
            for k in range(6):
                leo = p[k] - uu[k]
                l_ref[c, x, k] = leo
                mod = m[k] - 4.0 * fmag * s[k]
                lm.append(leo * mod)
                mm.append(mod * mod)
            lm_sum += lm[0] + lm[1] + lm[2] + 2.0 * (lm[3] + lm[4] + lm[5])
            mm_sum += mm[0] + mm[1] + mm[2] + 2.0 * (mm[3] + mm[4] + mm[5])
        hot = bins[1, pl.ds(pl.multiple_of(r0 + y0, 8), 8), :] == lanes
        num = sums[0] + jnp.where(hot, jnp.sum(lm_sum, axis=1, keepdims=True), 0.0)
        den = sums[1] + jnp.where(hot, jnp.sum(mm_sum, axis=1, keepdims=True), 0.0)
        return num, den

    zero = jnp.zeros((8, 128), F32)
    num, den = lax.fori_loop(0, 16, contract, (zero, zero))
    row = lax.broadcasted_iota(jnp.int32, (8, 128), 0)
    num = jnp.sum(num, axis=0, keepdims=True)
    den = jnp.sum(den, axis=0, keepdims=True)
    part_ref[...] = jnp.where(row == 0, num, jnp.where(row == 1, den, 0.0))


def give_back(l_ref, part_ref, o_ref, tot_ref, a1, a2, s1, ss1, rs1, ss2, rs2, sb, rb, local):
    px, pz, h, yy, xx = where_am_i()

    def peer(k):
        return ((h + k // 16) % 2) * 16 + ((yy + (k % 16) // 4) % 4) * 4 + (xx + k % 4) % 4

    barrier = pltpu.get_barrier_semaphore()
    for k in range(1, 32):
        pl.semaphore_signal(barrier, inc=1, device_id=(px, peer(k)), device_id_type=MESH)
    for k in range(1, 8):
        pl.semaphore_signal(barrier, inc=1, device_id=((px + k) % 8, pz), device_id_type=MESH)
    pl.semaphore_wait(barrier, 38)

    def small(k):
        return pltpu.make_async_remote_copy(
            src_ref=part_ref,
            dst_ref=a1.at[pz],
            send_sem=ss1.at[k],
            recv_sem=rs1.at[k],
            device_id=(px, peer(k)),
            device_id_type=MESH,
        )

    def second(k):
        return pltpu.make_async_remote_copy(
            src_ref=s1,
            dst_ref=a2.at[px],
            send_sem=ss2.at[k],
            recv_sem=rs2.at[k],
            device_id=((px + k) % 8, pz),
            device_id_type=MESH,
        )

    def big(k):
        return pltpu.make_async_remote_copy(
            src_ref=l_ref.at[peer(k) % 16],
            dst_ref=o_ref.at[pz % 16],
            send_sem=sb.at[k],
            recv_sem=rb.at[k],
            device_id=(px, peer(k)),
            device_id_type=MESH,
        )

    for k in range(1, 32):
        small(k).start()
    for k in range(1, 16):
        big(k).start()
    a1[pz] = part_ref[...]
    for k in range(1, 32):
        small(k).wait_recv()
    total = a1[0]
    for q in range(1, 32):
        total = total + a1[q]
    s1[...] = total
    a2[px] = total
    here = pltpu.make_async_copy(l_ref.at[pz % 16], o_ref.at[pz % 16], local.at[0])
    here.start()
    for k in range(1, 8):
        second(k).start()
    for k in range(1, 8):
        second(k).wait_recv()
    total = a2[0]
    for q in range(1, 8):
        total = total + a2[q]
    tot_ref[...] = total
    here.wait()
    for k in range(1, 32):
        small(k).wait_send()
    for k in range(1, 8):
        second(k).wait_send()
    for k in range(1, 16):
        big(k).wait()


def to_planes(tot_ref, pb_ref, o_ref, leo_ref, visc_ref, coef_ref, mix):
    pz = lax.axis_index("pz")
    per_bin = tot_ref[0:1, :] / jnp.maximum(tot_ref[1:2, :], 65536.0)
    per_bin = jnp.broadcast_to(per_bin, (128, 128)).T
    hot = lax.broadcasted_iota(jnp.int32, (128, 256), 0) == pb_ref[...]
    both = jnp.concatenate([per_bin, per_bin], axis=1)
    coef = jnp.sum(jnp.where(hot, both, 0.0), axis=0, keepdims=True)
    coef_ref[...] = coef
    at = lax.broadcasted_iota(jnp.int32, (1, 256), 1) - pz * 8
    low = lax.broadcasted_iota(jnp.int32, (64, 128), 1) < 64

    def plane(y, _):
        mine = jnp.sum(jnp.where(at == y, coef, 0.0), axis=1, keepdims=True)
        for f in range(7):
            m = o_ref[pl.ds(f * 8 + y, 64, stride=56), :]
            mix[f] = jnp.concatenate([m, m], axis=0).T
            v = jnp.where(low, mix[f, pl.ds(0, 64, stride=2), :], mix[f, pl.ds(1, 64, stride=2), :])
            if f < 6:
                leo_ref[f, y] = v
            else:
                visc_ref[y] = mine * v
        return 0

    lax.fori_loop(0, 8, plane, 0)


def spec(space):
    return pl.BlockSpec(memory_space=space)


def params(**kw):
    return pltpu.CompilerParams(vmem_limit_bytes=56 * 1024 * 1024, **kw)


DMA = pltpu.SemaphoreType.DMA


def local_step(velocity, filter_inverse, filter_block, plane_bin):
    edge = jax.ShapeDtypeStruct((48, 128), F32)
    rows, right, left = pl.pallas_call(
        to_columns,
        out_shape=(jax.ShapeDtypeStruct((68 * 24, 128), F32), edge, edge),
        in_specs=[spec(VMEM)],
        out_specs=(spec(VMEM),) * 3,
        scratch_shapes=[VMEM((3, 128, 128), F32)],
        compiler_params=params(),
        name="to_columns",
    )(velocity)
    below = lax.ppermute(right, "px", [(i, (i + 1) % 8) for i in range(8)])
    above = lax.ppermute(left, "px", [((i + 1) % 8, i) for i in range(8)])
    columns = pl.pallas_call(
        spread,
        out_shape=jax.ShapeDtypeStruct((8, 3, 256, 128), F32),
        in_specs=[spec(pl.ANY), spec(VMEM), spec(VMEM)],
        out_specs=spec(pl.ANY),
        scratch_shapes=[
            VMEM((68, 3, 8, 128), F32),
            VMEM((68, 3, 8, 128), F32),
            DMA((3,)),
            DMA((3,)),
            DMA((16,)),
            DMA((16,)),
            DMA((3, 16)),
            DMA((3, 16)),
            DMA((4,)),
        ],
        compiler_params=params(collective_id=0, has_side_effects=True),
        name="spread",
    )(rows.reshape(68, 3, 8, 128), below.reshape(2, 3, 8, 128), above.reshape(2, 3, 8, 128))
    bins = plane_bin.reshape(1, 256)
    leo, part = pl.pallas_call(
        math,
        out_shape=(
            jax.ShapeDtypeStruct((16, 4, 7, 8, 128), F32),
            jax.ShapeDtypeStruct((8, 128), F32),
        ),
        in_specs=[spec(VMEM)] * 4,
        out_specs=(spec(VMEM), spec(VMEM)),
        scratch_shapes=[
            VMEM((21, 6, 16, 128), F32),
            VMEM((21, 256, 512), BF16),
            VMEM((21, 256, 512), BF16),
            VMEM((21, 128, 512), F32),
            VMEM((128, 256), BF16),
            VMEM((128, 256), BF16),
            VMEM((2, 256, 128), jnp.int32),
        ],
        compiler_params=params(),
        name="math",
    )(columns, filter_inverse, filter_block.reshape(1, 256), bins)
    back, total = pl.pallas_call(
        give_back,
        out_shape=(
            jax.ShapeDtypeStruct((16, 4, 7, 8, 128), F32),
            jax.ShapeDtypeStruct((8, 128), F32),
        ),
        in_specs=[spec(VMEM)] * 2,
        out_specs=(spec(pl.ANY), spec(VMEM)),
        scratch_shapes=[
            VMEM((32, 8, 128), F32),
            VMEM((8, 8, 128), F32),
            VMEM((8, 128), F32),
            DMA((32,)),
            DMA((32,)),
            DMA((8,)),
            DMA((8,)),
            DMA((16,)),
            DMA((16,)),
            DMA((1,)),
        ],
        compiler_params=params(collective_id=1, has_side_effects=True),
        name="give_back",
    )(leo, part)
    leonard, viscosity, coefficient = pl.pallas_call(
        to_planes,
        out_shape=(
            jax.ShapeDtypeStruct((6, 8, 64, 128), F32),
            jax.ShapeDtypeStruct((8, 64, 128), F32),
            jax.ShapeDtypeStruct((1, 256), F32),
        ),
        in_specs=[spec(VMEM)] * 3,
        out_specs=(spec(VMEM),) * 3,
        scratch_shapes=[VMEM((7, 128, 128), F32)],
        compiler_params=params(),
        name="to_planes",
    )(total, bins, back.reshape(16 * 4 * 56, 128))
    return leonard, viscosity, coefficient.reshape(256)


def solution(mesh):
    return jax.shard_map(
        local_step,
        mesh=mesh,
        in_specs=(P(None, "pz", None, "px"), P(), P(), P()),
        out_specs=(P(None, "pz", None, "px"), P("pz", None, "px"), P()),
        check_vma=False,
    )
```

time: 142 us -> 134 us (0.944)
  the two profiles are of different devices: /device:TPU:104 before, /device:TPU:32 now
where the time goes in v2:
time: 134 us; the launch traced here: 133 us
  Pallas kernels  128 us (96%)
  starting transfers between devices  1.75 us (1%)
  waiting for transfers between devices  1.73 us (1%)
    pallas_call x1, Pallas kernels, local_step(): pl.pallas_call(spread, out_shape=jax.ShapeDtypeStruct((8, 3, 256, 128), F...  60 us
    pallas_call x1, Pallas kernels, local_step(): pl.pallas_call(give_back, out_shape=(jax.ShapeDtypeStruct((16, 4, 7, 8, 1...  34.9 us
    pallas_call x1, Pallas kernels, local_step(): pl.pallas_call(math, out_shape=(jax.ShapeDtypeStruct((16, 4, 7, 8, 128),...  24.7 us
    pallas_call x1, Pallas kernels, local_step(): pl.pallas_call(to_planes, out_shape=(jax.ShapeDtypeStruct((6, 8, 64, 128)...  4.94 us
    pallas_call x1, Pallas kernels, local_step(): pl.pallas_call(to_columns, out_shape=(jax.ShapeDtypeStruct((68 * 24, 128)...  3.31 us
  transfers between devices with their start and end apart: 2, of which 1 were waited for; matrix products, arithmetic and copies ran while one was open for 0% of the time, Pallas kernels for 0%

profile of v2, /device:TPU:32, one launch (start us, length us, event | category | flops | bytes accessed | tf_op | source)
XLA Modules:
  0.0 132.6 jit_solution(13674630841561476927)
XLA Ops:
  0.6 3.3 %to_columns.1 = (f32[1632,128]{1,0:T(8,128)}, f32[48,128]{1,0:T(8,128)}, f32[48,128]{1,0:T(8,128)}) custom-call(f32[3,8,64,128]{3,2,1,0:T(8,128)} %vel_ref.1), custom_call_target="tpu_custom_call" | custom-call | tf_op jit(solution)/shard_map/to_columns/pallas_call | solution.py:357
  3.9 0.0 collective-permute-start
  3.9 1.7 %collective-permute-start.1 = (f32[48,128]{1,0:T(8,128)}, f32[48,128]{1,0:T(8,128)S(1)}, u32[]{:S(2)}, u32[]{:S(2)}) collective-permute-start(f32[48,128]{1,0:T(8,128)} %get-tuple-element.15), channel_id=1, source_target_pairs={{32,0},{64,32},{96,64},{128,96},{160,128},{192,160},{224,192},{0,2... | collective-permute-start | bytes 73736 | tf_op jit(solution)/shard_map/ppermute | solution.py:367
  5.7 1.7 %collective-permute-done = f32[48,128]{1,0:T(8,128)S(1)} collective-permute-done((f32[48,128]{1,0:T(8,128)}, f32[48,128]{1,0:T(8,128)S(1)}, u32[]{:S(2)}, u32[]{:S(2)}) %collective-permute-start) | collective-permute-done | bytes 24608 | tf_op jit(solution)/shard_map/ppermute | solution.py:366
  7.4 0.0 copy-start
  7.4 0.0 collective-permute-done.1
  7.4 0.0 copy-start.1
  7.4 0.6 copy-done
  8.0 0.0 copy-done.1
  8.0 60.0 %spread.1.r_ref = f32[8,3,256,128]{3,2,1,0:T(8,128)} custom-call(f32[68,3,8,128]{3,2,1,0:T(8,128)} %bitcast.8, f32[2,3,8,128]{3,2,1,0:T(8,128)} %bitcast.9, f32[2,3,8,128]{3,2,1,0:T(8,128)} %bitcast.10), custom_call_target="tpu_custom_call" | custom-call | tf_op jit(solution)/shard_map/spread/pallas_call | solution.py:368
  68.1 24.7 %math.1 = (f32[16,4,7,8,128]{4,3,2,1,0:T(8,128)}, f32[8,128]{1,0:T(8,128)}) custom-call(f32[8,3,256,128]{3,2,1,0:T(8,128)} %spread.1.r_ref, f32[256,256]{1,0:T(8,128)} %inv_ref.1, s32[1,256]{1,0:T(1,128)} %bitcast.13, s32[1,256]{1,0:T(1,128)} %bitcast.11), custom_call_target="tpu_custom_call" | custom-call | tf_op jit(solution)/shard_map/math/pallas_call | solution.py:388
  92.7 34.9 %give_back.1 = (f32[16,4,7,8,128]{4,3,2,1,0:T(8,128)}, f32[8,128]{1,0:T(8,128)}) custom-call(f32[16,4,7,8,128]{4,3,2,1,0:T(8,128)} %get-tuple-element.16.l_ref, f32[8,128]{1,0:T(8,128)} %get-tuple-element.17.part_ref), custom_call_target="tpu_custom_call" | custom-call | tf_op jit(solution)/shard_map/give_back/pallas_call | solution.py:408
  127.6 4.9 %to_planes.1 = (f32[6,8,64,128]{3,2,1,0:T(8,128)}, f32[8,64,128]{2,1,0:T(8,128)}, f32[1,256]{1,0:T(1,128)}) custom-call(f32[8,128]{1,0:T(8,128)} %get-tuple-element.18.tot_ref, s32[1,256]{1,0:T(1,128)} %bitcast.12, f32[3584,128]{1,0:T(8,128)} %bitcast.7), custom_call_target="tpu_custom_call" | custom-call | tf_op jit(solution)/shard_map/to_planes/pallas_call | solution.py:431
Async XLA Ops:
  3.9 3.5 %collective-permute-start = (f32[48,128]{1,0:T(8,128)}, f32[48,128]{1,0:T(8,128)S(1)}, u32[]{:S(2)}, u32[]{:S(2)}) collective-permute-start(f32[48,128]{1,0:T(8,128)} %get-tuple-element.14), channel_id=1, source_target_pairs={{0,32},{32,64},{64,96},{96,128},{128,160},{160,192},{192,224},{224... | collective-permute-start | bytes 73736 | tf_op jit(solution)/shard_map/ppermute | solution.py:366
  3.9 3.5 %collective-permute-start.1 = (f32[48,128]{1,0:T(8,128)}, f32[48,128]{1,0:T(8,128)S(1)}, u32[]{:S(2)}, u32[]{:S(2)}) collective-permute-start(f32[48,128]{1,0:T(8,128)} %get-tuple-element.15), channel_id=1, source_target_pairs={{32,0},{64,32},{96,64},{128,96},{160,128},{192,160},{224,192},{0,2... | collective-permute-start | bytes 73736 | tf_op jit(solution)/shard_map/ppermute | solution.py:367
  7.4 0.6 copy-start
  7.4 0.6 copy-start.1

commit v3 on v2

--- a/solution.py
+++ b/solution.py
@@ -30,6 +30,9 @@
     x_ref[66 * 24 : 68 * 24, :] = pltpu.roll(first, 127, 1)
     right_ref[...] = pltpu.roll(last, 127, 1)
     left_ref[...] = pltpu.roll(first, 1, 1)
+
+
+ORDER = (10, 6, 14, 8, 9, 11, 2, 5, 15, 13, 7, 1, 3, 4, 12)
 
 
 def where_am_i():
@@ -95,7 +98,7 @@
 
     for f in range(3):
         across(f).start()
-    for k in range(1, 16):
+    for k in ORDER:
         own(k).start()
     here = pltpu.make_async_copy(
         rows.at[pl.ds(i * 4, 8)],
@@ -105,7 +108,7 @@
     here.start()
     for f in range(3):
         across(f).wait_recv()
-        for k in range(1, 16):
+        for k in ORDER:
             theirs(f, k).start()
         there(f).start()
     here.wait()
@@ -286,7 +289,7 @@
 
     for k in range(1, 32):
         small(k).start()
-    for k in range(1, 16):
+    for k in ORDER:
         big(k).start()
     a1[pz] = part_ref[...]
     for k in range(1, 32):

time: 134 us -> 131 us (0.978)
  Pallas kernels: 128 us -> 124 us
    pallas_call x1, Pallas kernels: 34.9 us -> 32.1 us  [local_step(): pl.pallas_call(give_back, out_shape=(jax.ShapeDtypeStruct((16, 4, 7, 8, 1...]
where the time goes in v3:
time: 131 us; the launch traced here: 129 us
  Pallas kernels  124 us (95%)
  starting transfers between devices  1.75 us (1%)
  waiting for transfers between devices  1.73 us (1%)
    pallas_call x1, Pallas kernels, local_step(): pl.pallas_call(spread, out_shape=jax.ShapeDtypeStruct((8, 3, 256, 128), F...  58.9 us
    pallas_call x1, Pallas kernels, local_step(): pl.pallas_call(give_back, out_shape=(jax.ShapeDtypeStruct((16, 4, 7, 8, 1...  32.1 us
    pallas_call x1, Pallas kernels, local_step(): pl.pallas_call(math, out_shape=(jax.ShapeDtypeStruct((16, 4, 7, 8, 128),...  24.7 us
    pallas_call x1, Pallas kernels, local_step(): pl.pallas_call(to_planes, out_shape=(jax.ShapeDtypeStruct((6, 8, 64, 128)...  4.94 us
    pallas_call x1, Pallas kernels, local_step(): pl.pallas_call(to_columns, out_shape=(jax.ShapeDtypeStruct((68 * 24, 128)...  3.31 us
  transfers between devices with their start and end apart: 2, of which 1 were waited for; matrix products, arithmetic and copies ran while one was open for 0% of the time, Pallas kernels for 0%

profile of v3, /device:TPU:32, one launch (start us, length us, event | category | flops | bytes accessed | tf_op | source)
XLA Modules:
  0.0 128.6 jit_solution(10607951937293616759)
XLA Ops:
  0.6 3.3 %to_columns.1 = (f32[1632,128]{1,0:T(8,128)}, f32[48,128]{1,0:T(8,128)}, f32[48,128]{1,0:T(8,128)}) custom-call(f32[3,8,64,128]{3,2,1,0:T(8,128)} %vel_ref.1), custom_call_target="tpu_custom_call" | custom-call | tf_op jit(solution)/shard_map/to_columns/pallas_call | solution.py:360
  3.9 0.0 collective-permute-start
  3.9 1.7 %collective-permute-start.1 = (f32[48,128]{1,0:T(8,128)}, f32[48,128]{1,0:T(8,128)S(1)}, u32[]{:S(2)}, u32[]{:S(2)}) collective-permute-start(f32[48,128]{1,0:T(8,128)} %get-tuple-element.15), channel_id=1, source_target_pairs={{32,0},{64,32},{96,64},{128,96},{160,128},{192,160},{224,192},{0,2... | collective-permute-start | bytes 73736 | tf_op jit(solution)/shard_map/ppermute | solution.py:370
  5.7 1.7 %collective-permute-done = f32[48,128]{1,0:T(8,128)S(1)} collective-permute-done((f32[48,128]{1,0:T(8,128)}, f32[48,128]{1,0:T(8,128)S(1)}, u32[]{:S(2)}, u32[]{:S(2)}) %collective-permute-start) | collective-permute-done | bytes 24608 | tf_op jit(solution)/shard_map/ppermute | solution.py:369
  7.4 0.0 copy-start
  7.4 0.0 collective-permute-done.1
  7.4 0.0 copy-start.1
  7.4 0.6 copy-done
  8.0 0.0 copy-done.1
  8.0 58.9 %spread.1.r_ref = f32[8,3,256,128]{3,2,1,0:T(8,128)} custom-call(f32[68,3,8,128]{3,2,1,0:T(8,128)} %bitcast.8, f32[2,3,8,128]{3,2,1,0:T(8,128)} %bitcast.9, f32[2,3,8,128]{3,2,1,0:T(8,128)} %bitcast.10), custom_call_target="tpu_custom_call" | custom-call | tf_op jit(solution)/shard_map/spread/pallas_call | solution.py:371
  66.9 24.7 %math.1 = (f32[16,4,7,8,128]{4,3,2,1,0:T(8,128)}, f32[8,128]{1,0:T(8,128)}) custom-call(f32[8,3,256,128]{3,2,1,0:T(8,128)} %spread.1.r_ref, f32[256,256]{1,0:T(8,128)} %inv_ref.1, s32[1,256]{1,0:T(1,128)} %bitcast.13, s32[1,256]{1,0:T(1,128)} %bitcast.11), custom_call_target="tpu_custom_call" | custom-call | tf_op jit(solution)/shard_map/math/pallas_call | solution.py:391
  91.6 32.1 %give_back.1 = (f32[16,4,7,8,128]{4,3,2,1,0:T(8,128)}, f32[8,128]{1,0:T(8,128)}) custom-call(f32[16,4,7,8,128]{4,3,2,1,0:T(8,128)} %get-tuple-element.16.l_ref, f32[8,128]{1,0:T(8,128)} %get-tuple-element.17.part_ref), custom_call_target="tpu_custom_call" | custom-call | tf_op jit(solution)/shard_map/give_back/pallas_call | solution.py:411
  123.7 4.9 %to_planes.1 = (f32[6,8,64,128]{3,2,1,0:T(8,128)}, f32[8,64,128]{2,1,0:T(8,128)}, f32[1,256]{1,0:T(1,128)}) custom-call(f32[8,128]{1,0:T(8,128)} %get-tuple-element.18.tot_ref, s32[1,256]{1,0:T(1,128)} %bitcast.12, f32[3584,128]{1,0:T(8,128)} %bitcast.7), custom_call_target="tpu_custom_call" | custom-call | tf_op jit(solution)/shard_map/to_planes/pallas_call | solution.py:434
Async XLA Ops:
  3.9 3.5 %collective-permute-start = (f32[48,128]{1,0:T(8,128)}, f32[48,128]{1,0:T(8,128)S(1)}, u32[]{:S(2)}, u32[]{:S(2)}) collective-permute-start(f32[48,128]{1,0:T(8,128)} %get-tuple-element.14), channel_id=1, source_target_pairs={{0,32},{32,64},{64,96},{96,128},{128,160},{160,192},{192,224},{224... | collective-permute-start | bytes 73736 | tf_op jit(solution)/shard_map/ppermute | solution.py:369
  3.9 3.5 %collective-permute-start.1 = (f32[48,128]{1,0:T(8,128)}, f32[48,128]{1,0:T(8,128)S(1)}, u32[]{:S(2)}, u32[]{:S(2)}) collective-permute-start(f32[48,128]{1,0:T(8,128)} %get-tuple-element.15), channel_id=1, source_target_pairs={{32,0},{64,32},{96,64},{128,96},{160,128},{192,160},{224,192},{0,2... | collective-permute-start | bytes 73736 | tf_op jit(solution)/shard_map/ppermute | solution.py:370
  7.4 0.6 copy-start
  7.4 0.6 copy-start.1

commit v4 on v3

v4 whole, which is shorter than its diff:
```python
import functools

import jax
import jax.numpy as jnp
from jax import lax
from jax.experimental import pallas as pl
from jax.experimental.pallas import tpu as pltpu
from jax.sharding import PartitionSpec as P

NBIN = 64
MESH = pl.DeviceIdType.MESH
F32 = jnp.float32
BF16 = jnp.bfloat16
VMEM = pltpu.VMEM
def to_columns(vel_ref, x_ref, right_ref, left_ref, mix):
    even = lax.broadcasted_iota(jnp.int32, (64, 128), 1) % 2 == 0

    def plane(y, _):
        for f in range(3):
            v = vel_ref[f, y]
            mix[f, pl.ds(0, 64, stride=2), :] = v
            mix[f, pl.ds(1, 64, stride=2), :] = v
            t = mix[f].T
            x_ref[pl.ds(48 + f * 8 + y, 64, stride=24), :] = jnp.where(even, t[:64], t[64:])
        return 0

    lax.fori_loop(0, 8, plane, 0)
    first, last = x_ref[48:96, :], x_ref[64 * 24 : 66 * 24, :]
    x_ref[0:48, :] = pltpu.roll(last, 1, 1)
    x_ref[66 * 24 : 68 * 24, :] = pltpu.roll(first, 127, 1)
    right_ref[...] = pltpu.roll(last, 127, 1)
    left_ref[...] = pltpu.roll(first, 1, 1)


ORDER = (10, 6, 14, 8, 9, 11, 2, 5, 15, 13, 7, 1, 3, 4, 12)


def where_am_i():
    px, pz = lax.axis_index("px"), lax.axis_index("pz")
    return px, pz, pz // 16, (pz % 16) // 4, pz % 4


def fields_of(u, gx, up, down):
    def d_x(f):
        return u[f][gx + 1] - u[f][gx - 1]

    def d_z(f):
        return pltpu.roll(u[f][gx], 126, 1) - pltpu.roll(u[f][gx], 2, 1)

    def d_y(f):
        return up[f] - down[f]

    t = [d_x(0), d_y(1), d_z(2), d_y(0) + d_x(1), d_z(0) + d_x(2), d_z(1) + d_y(2)]
    mag = twice_norm(t)
    a, b, c = u[0][gx], u[1][gx], u[2][gx]
    return [a, b, c] + t + [a * a, b * b, c * c, a * b, a * c, b * c] + [mag * q for q in t], mag


def twice_norm(t):
    return jnp.sqrt(
        2.0 * (t[0] * t[0] + t[1] * t[1] + t[2] * t[2]) + (t[3] * t[3] + t[4] * t[4] + t[5] * t[5])
    )


def column(row):
    return jnp.broadcast_to(row, (128, 256)).T


def core(
    x_ref, below_ref, above_ref, inv_ref, fb_ref, pb_ref, o_ref, tot_ref,
    rows, partner, r, g, bh, bl, ff, ww, bins, leo, part, a1, a2, s1,
    send_a, recv_a, send_b, recv_b, send_c, recv_c, ss1, rs1, ss2, rs2, sb, rb, local,
):
    px, pz, h, yy, xx = where_am_i()
    i = pz % 16
    other = 1 - h

    def mate(k):
        return ((yy + k // 4) % 4) * 4 + (xx + k % 4) % 4

    def peer(k):
        return ((h + k // 16) % 2) * 16 + mate(k % 16)

    def send(src, dst, sems, recvs, where):
        return pltpu.make_async_remote_copy(
            src_ref=src, dst_ref=dst, send_sem=sems, recv_sem=recvs, device_id=where, device_id_type=MESH
        )

    fetch = pltpu.make_async_copy(x_ref, rows, local.at[0])
    fetch.start()
    barrier = pltpu.get_barrier_semaphore()
    for k in range(1, 32):
        pl.semaphore_signal(barrier, inc=1, device_id=(px, peer(k)), device_id_type=MESH)
    for k in range(1, 8):
        pl.semaphore_signal(barrier, inc=1, device_id=((px + k) % 8, pz), device_id_type=MESH)
    fetch.wait()
    even = lax.broadcasted_iota(jnp.int32, (2, 3, 8, 128), 3) % 2 == 0
    rows[0:2] = jnp.where(even, below_ref[...], rows[0:2])
    rows[66:68] = jnp.where(even, rows[66:68], above_ref[...])
    pl.semaphore_wait(barrier, 38)

    own_planes = pl.ds(pl.multiple_of(pz * 8, 8), 8)
    their_planes = pl.ds(pl.multiple_of((other * 16 + i) * 8, 8), 8)

    def across(f):
        return send(rows.at[:, f], partner.at[:, f], send_a.at[f], recv_a.at[f], (px, other * 16 + i))

    def own(k):
        return send(
            rows.at[pl.ds(mate(k) * 4, 8)], r.at[:, :, own_planes, :],
            send_b.at[k], recv_b.at[k], (px, h * 16 + mate(k)),
        )

    def theirs(f, k):
        return send(
            partner.at[pl.ds(mate(k) * 4, 8), f], r.at[:, f, their_planes, :],
            send_c.at[f, k], recv_c.at[f, k], (px, h * 16 + mate(k)),
        )

    def there(f):
        return pltpu.make_async_copy(partner.at[pl.ds(i * 4, 8), f], r.at[:, f, their_planes, :], local.at[1 + f])

    for f in range(3):
        across(f).start()
    for k in ORDER:
        own(k).start()
    here = pltpu.make_async_copy(rows.at[pl.ds(i * 4, 8)], r.at[:, :, own_planes, :], local.at[0])
    here.start()

    r0 = pl.multiple_of(h * 128, 128)
    bins[0] = column(fb_ref[...])
    bins[1] = column(pb_ref[...])
    mine = bins[0, pl.ds(r0, 128), :]
    masked = jnp.where(jnp.concatenate([mine, mine], axis=1) == fb_ref[...], inv_ref[pl.ds(r0, 128), :], 0.0)
    w = masked / jnp.sum(masked, axis=1, keepdims=True) * 0.0625
    w_hi = w.astype(BF16)
    ww[0:128, :] = w_hi
    ww[128:256, :] = (w - w_hi.astype(F32)).astype(BF16)

    def strip(c, mags):
        y0 = pl.multiple_of(c * 16, 16)
        before = pl.multiple_of(jnp.maximum(y0 - 8, 0), 8)
        after = pl.multiple_of(jnp.minimum(y0 + 16, 248), 8)
        first, last = c == 0, c == 15
        u = [[r[x, f, pl.ds(y0, 16), :] for x in range(8)] for f in range(3)]
        for gx in range(1, 7):
            up, down = [], []
            for f in range(3):
                prev = jnp.where(first, 0.0, r[gx, f, pl.ds(before, 8), :])
                succ = jnp.where(last, 0.0, r[gx, f, pl.ds(after, 8), :])
                down.append(jnp.concatenate([prev[7:], u[f][gx][:15]], axis=0))
                up.append(jnp.concatenate([u[f][gx][1:], succ[:1]], axis=0))
            out, mag = fields_of(u, gx, up, down)
            for k in range(21):
                g[k, gx - 1] = out[k]
            if 2 <= gx <= 5:
                mags(c, gx - 2, mag)
        for k in range(21):
            gs = [g[k, t] for t in range(6)]
            pairs = [gs[t] + gs[t + 1] for t in range(5)]
            for x in range(4):
                total = pairs[x] + pairs[x + 1]
                total = total + pltpu.roll(total, 2, 1)
                box = total + pltpu.roll(total, 126, 1)
                hi = box.astype(BF16)
                bh[k, pl.ds(y0, 16), pl.ds(x * 128, 128)] = hi
                bl[k, pl.ds(y0, 16), pl.ds(x * 128, 128)] = (box - hi.astype(F32)).astype(BF16)

    def keep(c, x, mag):
        block = 2 * c - 16 * h
        leo[block, x, 6] = mag[:8]
        leo[block + 1, x, 6] = mag[8:]

    def keep_own(c, x, mag):
        @pl.when(c // 8 == h)
        def _():
            keep(jnp.clip(c, 8 * h, 8 * h + 7), x, mag)

    def early(t, _):
        strip(9 * h + t, keep)
        return 0

    def late(t, _):
        strip(7 * other + t, keep_own)
        return 0

    across(0).wait_recv()
    for k in ORDER:
        theirs(0, k).start()
    there(0).start()
    here.wait()
    for k in range(1, 16):
        own(k).wait_recv()
    lax.fori_loop(0, 7, early, 0)
    for f in (1, 2):
        across(f).wait_recv()
        for k in ORDER:
            theirs(f, k).start()
        there(f).start()
    for f in range(3):
        there(f).wait()
        for k in range(1, 16):
            theirs(f, k).wait_recv()
    lax.fori_loop(0, 9, late, 0)

    lanes = lax.broadcasted_iota(jnp.int32, (8, 128), 1)

    def products(x0):
        def product(q, _):
            for t in range(3):
                k = q * 3 + t
                hi = bh[k, :, pl.ds(x0 * 128, 256)]
                lo = bl[k, :, pl.ds(x0 * 128, 256)]
                both = jnp.dot(ww[...], hi, preferred_element_type=F32)
                rest = jnp.dot(ww[0:128, :], lo, preferred_element_type=F32)
                ff[k] = both[:128] + (both[128:] + rest)
            return 0

        lax.fori_loop(0, 7, product, 0)

    def contracts(x0, sums):
        def contract(c, sums):
            y0 = pl.multiple_of(c * 8, 8)
            lm_sum, mm_sum = 0.0, 0.0
            for x in range(2):
                f = [ff[k, pl.ds(y0, 8), pl.ds(x * 128, 128)] for k in range(21)]
                a, b, d = f[0], f[1], f[2]
                t, p, m = f[3:9], f[9:15], f[15:21]
                uu = [a * a, b * b, d * d, a * b, a * d, b * d]
                fmag = 4.0 * twice_norm(t)
                lm, mm = [], []
                for k in range(6):
                    stress = p[k] - uu[k]
                    leo[c, x0 + x, k] = stress
                    mod = m[k] - fmag * t[k]
                    lm.append(stress * mod)
                    mm.append(mod * mod)
                lm_sum += lm[0] + lm[1] + lm[2] + lm[3] + lm[4] + lm[5]
                mm_sum += 2.0 * (mm[0] + mm[1] + mm[2]) + (mm[3] + mm[4] + mm[5])
            hot = bins[1, pl.ds(pl.multiple_of(r0 + y0, 8), 8), :] == lanes
            num = sums[0] + jnp.where(hot, jnp.sum(lm_sum, axis=1, keepdims=True), 0.0)
            den = sums[1] + jnp.where(hot, jnp.sum(mm_sum, axis=1, keepdims=True), 0.0)
            return num, den

        return lax.fori_loop(0, 16, contract, sums)

    def big(half, k):
        return send(
            leo.at[mate(k), pl.ds(half * 2, 2)], o_ref.at[i, pl.ds(half * 2, 2)],
            sb.at[half, k], rb.at[half, k], (px, h * 16 + mate(k)),
        )

    def small(k):
        return send(part, a1.at[pz], ss1.at[k], rs1.at[k], (px, peer(k)))

    def second(k):
        return send(s1, a2.at[px], ss2.at[k], rs2.at[k], ((px + k) % 8, pz))

    zero = jnp.zeros((8, 128), F32)
    products(0)
    sums = contracts(0, (zero, zero))
    products(2)
    for k in ORDER:
        big(0, k).start()
    num, den = contracts(2, sums)
    row = lax.broadcasted_iota(jnp.int32, (8, 128), 0)
    num = jnp.sum(num, axis=0, keepdims=True) * 0.25
    den = jnp.sum(den, axis=0, keepdims=True) * 0.03125
    mine = jnp.where(row == 0, num, jnp.where(row == 1, den, 0.0))
    part[...] = mine
    a1[pz] = mine
    for f in range(3):
        across(f).wait_send()
        for k in range(1, 16):
            theirs(f, k).wait_send()
    for k in range(1, 16):
        own(k).wait_send()
    for k in range(1, 32):
        small(k).start()
    for k in ORDER:
        big(1, k).start()
    keep_here = pltpu.make_async_copy(leo.at[i], o_ref.at[i], local.at[0])
    keep_here.start()
    for k in range(1, 32):
        small(k).wait_recv()
    total = a1[0]
    for q in range(1, 32):
        total = total + a1[q]
    s1[...] = total
    a2[px] = total
    for k in range(1, 32):
        small(k).wait_send()
    for k in range(1, 8):
        second(k).start()
    for k in range(1, 8):
        second(k).wait_recv()
    total = a2[0]
    for q in range(1, 8):
        total = total + a2[q]
    tot_ref[...] = total
    keep_here.wait()
    for k in range(1, 8):
        second(k).wait_send()
    for half in range(2):
        for k in range(1, 16):
            big(half, k).wait()


def to_planes(tot_ref, pb_ref, o_ref, leo_ref, visc_ref, coef_ref, mix):
    pz = lax.axis_index("pz")
    per_bin = tot_ref[0:1, :] / jnp.maximum(tot_ref[1:2, :], 65536.0)
    per_bin = jnp.broadcast_to(per_bin, (128, 128)).T
    hot = lax.broadcasted_iota(jnp.int32, (128, 256), 0) == pb_ref[...]
    both = jnp.concatenate([per_bin, per_bin], axis=1)
    coef = jnp.sum(jnp.where(hot, both, 0.0), axis=0, keepdims=True)
    coef_ref[...] = coef
    at = lax.broadcasted_iota(jnp.int32, (1, 256), 1) - pz * 8
    low = lax.broadcasted_iota(jnp.int32, (64, 128), 1) < 64

    def plane(y, _):
        mine = jnp.sum(jnp.where(at == y, coef, 0.0), axis=1, keepdims=True)
        for f in range(7):
            m = o_ref[pl.ds(f * 8 + y, 64, stride=56), :]
            mix[f] = jnp.concatenate([m, m], axis=0).T
            v = jnp.where(low, mix[f, pl.ds(0, 64, stride=2), :], mix[f, pl.ds(1, 64, stride=2), :])
            if f < 6:
                leo_ref[f, y] = v
            else:
                visc_ref[y] = mine * 0.5 * v
        return 0

    lax.fori_loop(0, 8, plane, 0)


def spec(space):
    return pl.BlockSpec(memory_space=space)


def params(**kw):
    return pltpu.CompilerParams(vmem_limit_bytes=56 * 1024 * 1024, **kw)


DMA = pltpu.SemaphoreType.DMA


def local_step(velocity, filter_inverse, filter_block, plane_bin):
    edge = jax.ShapeDtypeStruct((48, 128), F32)
    rows, right, left = pl.pallas_call(
        to_columns,
        out_shape=(jax.ShapeDtypeStruct((68 * 24, 128), F32), edge, edge),
        in_specs=[spec(VMEM)],
        out_specs=(spec(VMEM),) * 3,
        scratch_shapes=[VMEM((3, 128, 128), F32)],
        compiler_params=params(),
        name="to_columns",
    )(velocity)
    below = lax.ppermute(right, "px", [(i, (i + 1) % 8) for i in range(8)])
    above = lax.ppermute(left, "px", [((i + 1) % 8, i) for i in range(8)])
    bins = plane_bin.reshape(1, 256)
    part = VMEM((68, 3, 8, 128), F32)
    back, total = pl.pallas_call(
        core,
        out_shape=(
            jax.ShapeDtypeStruct((16, 4, 7, 8, 128), F32),
            jax.ShapeDtypeStruct((8, 128), F32),
        ),
        in_specs=[spec(pl.ANY)] + [spec(VMEM)] * 5,
        out_specs=(spec(pl.ANY), spec(VMEM)),
        scratch_shapes=[
            part,
            part,
            VMEM((8, 3, 256, 128), F32),
            VMEM((21, 6, 16, 128), F32),
            VMEM((21, 256, 512), BF16),
            VMEM((21, 256, 512), BF16),
            VMEM((21, 128, 256), F32),
            VMEM((256, 256), BF16),
            VMEM((2, 256, 128), jnp.int32),
            VMEM((16, 4, 7, 8, 128), F32),
            VMEM((8, 128), F32),
            VMEM((32, 8, 128), F32),
            VMEM((8, 8, 128), F32),
            VMEM((8, 128), F32),
            DMA((3,)),
            DMA((3,)),
            DMA((16,)),
            DMA((16,)),
            DMA((3, 16)),
            DMA((3, 16)),
            DMA((32,)),
            DMA((32,)),
            DMA((8,)),
            DMA((8,)),
            DMA((2, 16)),
            DMA((2, 16)),
            DMA((4,)),
        ],
        compiler_params=params(collective_id=0, has_side_effects=True),
        name="core",
    )(
        rows.reshape(68, 3, 8, 128),
        below.reshape(2, 3, 8, 128),
        above.reshape(2, 3, 8, 128),
        filter_inverse,
        filter_block.reshape(1, 256),
        bins,
    )
    leonard, viscosity, coefficient = pl.pallas_call(
        to_planes,
        out_shape=(
            jax.ShapeDtypeStruct((6, 8, 64, 128), F32),
            jax.ShapeDtypeStruct((8, 64, 128), F32),
            jax.ShapeDtypeStruct((1, 256), F32),
        ),
        in_specs=[spec(VMEM)] * 3,
        out_specs=(spec(VMEM),) * 3,
        scratch_shapes=[VMEM((7, 128, 128), F32)],
        compiler_params=params(),
        name="to_planes",
    )(total, bins, back.reshape(16 * 4 * 56, 128))
    return leonard, viscosity, coefficient.reshape(256)


def solution(mesh):
    return jax.shard_map(
        local_step,
        mesh=mesh,
        in_specs=(P(None, "pz", None, "px"), P(), P(), P()),
        out_specs=(P(None, "pz", None, "px"), P("pz", None, "px"), P()),
        check_vma=False,
    )
```

time: 131 us -> 169 us (1.29)
  Pallas kernels: 124 us -> 161 us
    pallas_call x3 -> x1, Pallas kernels: 116 us -> 153 us  [local_step(): pl.pallas_call(core, out_shape=(jax.ShapeDtypeStruct((16, 4, 7, 8, 128),...]
where the time goes in v4:
time: 169 us; the launch traced here: 166 us
  Pallas kernels  161 us (95%)
  starting transfers between devices  1.75 us (1%)
  waiting for transfers between devices  1.73 us (1%)
    pallas_call x1, Pallas kernels, local_step(): pl.pallas_call(core, out_shape=(jax.ShapeDtypeStruct((16, 4, 7, 8, 128),...  153 us
    pallas_call x1, Pallas kernels, local_step(): pl.pallas_call(to_planes, out_shape=(jax.ShapeDtypeStruct((6, 8, 64, 128)...  4.94 us
  transfers between devices with their start and end apart: 2, of which 1 were waited for; matrix products, arithmetic and copies ran while one was open for 0% of the time, Pallas kernels for 0%

profile of v4, /device:TPU:32, one launch (start us, length us, event | category | flops | bytes accessed | tf_op | source)
XLA Modules:
  0.0 166.1 jit_solution(9769531984612698479)
XLA Ops:
  0.6 3.3 %to_columns.1 = (f32[1632,128]{1,0:T(8,128)}, f32[48,128]{1,0:T(8,128)}, f32[48,128]{1,0:T(8,128)}) custom-call(f32[3,8,64,128]{3,2,1,0:T(8,128)} %vel_ref.1), custom_call_target="tpu_custom_call" | custom-call | tf_op jit(solution)/shard_map/to_columns/pallas_call | solution.py:348
  3.9 0.0 collective-permute-start
  3.9 1.7 %collective-permute-start.1 = (f32[48,128]{1,0:T(8,128)}, f32[48,128]{1,0:T(8,128)S(1)}, u32[]{:S(2)}, u32[]{:S(2)}) collective-permute-start(f32[48,128]{1,0:T(8,128)} %get-tuple-element.13), channel_id=1, source_target_pairs={{32,0},{64,32},{96,64},{128,96},{160,128},{192,160},{224,192},{0,2... | collective-permute-start | bytes 73736 | tf_op jit(solution)/shard_map/ppermute | solution.py:358
  5.7 1.7 %collective-permute-done = f32[48,128]{1,0:T(8,128)S(1)} collective-permute-done((f32[48,128]{1,0:T(8,128)}, f32[48,128]{1,0:T(8,128)S(1)}, u32[]{:S(2)}, u32[]{:S(2)}) %collective-permute-start) | collective-permute-done | bytes 24608 | tf_op jit(solution)/shard_map/ppermute | solution.py:357
  7.4 0.0 copy-start
  7.4 0.0 collective-permute-done.1
  7.4 0.0 copy-start.1
  7.4 0.6 copy-done
  8.0 0.0 copy-done.1
  8.0 153.2 %core.1 = (f32[16,4,7,8,128]{4,3,2,1,0:T(8,128)}, f32[8,128]{1,0:T(8,128)}) custom-call(f32[68,3,8,128]{3,2,1,0:T(8,128)} %bitcast.8, f32[2,3,8,128]{3,2,1,0:T(8,128)} %bitcast.9, f32[2,3,8,128]{3,2,1,0:T(8,128)} %bitcast.10, f32[256,256]{1,0:T(8,128)} %inv_ref.1, s32[1,256]{1,0:T(1,128)} %bitcast.13, s32[1,256]{1,0:T(1,128)} %bitcast.11), custom_call_target="tpu_custom_call" | custom-call | tf_op jit(solution)/shard_map/core/pallas_call | solution.py:361
  161.2 4.9 %to_planes.1 = (f32[6,8,64,128]{3,2,1,0:T(8,128)}, f32[8,64,128]{2,1,0:T(8,128)}, f32[1,256]{1,0:T(1,128)}) custom-call(f32[8,128]{1,0:T(8,128)} %get-tuple-element.14.tot_ref, s32[1,256]{1,0:T(1,128)} %bitcast.12, f32[3584,128]{1,0:T(8,128)} %bitcast.7), custom_call_target="tpu_custom_call" | custom-call | tf_op jit(solution)/shard_map/to_planes/pallas_call | solution.py:408
Async XLA Ops:
  3.9 3.5 %collective-permute-start = (f32[48,128]{1,0:T(8,128)}, f32[48,128]{1,0:T(8,128)S(1)}, u32[]{:S(2)}, u32[]{:S(2)}) collective-permute-start(f32[48,128]{1,0:T(8,128)} %get-tuple-element.12), channel_id=1, source_target_pairs={{0,32},{32,64},{64,96},{96,128},{128,160},{160,192},{192,224},{224... | collective-permute-start | bytes 73736 | tf_op jit(solution)/shard_map/ppermute | solution.py:357
  3.9 3.5 %collective-permute-start.1 = (f32[48,128]{1,0:T(8,128)}, f32[48,128]{1,0:T(8,128)S(1)}, u32[]{:S(2)}, u32[]{:S(2)}) collective-permute-start(f32[48,128]{1,0:T(8,128)} %get-tuple-element.13), channel_id=1, source_target_pairs={{32,0},{64,32},{96,64},{128,96},{160,128},{192,160},{224,192},{0,2... | collective-permute-start | bytes 73736 | tf_op jit(solution)/shard_map/ppermute | solution.py:358
  7.4 0.6 copy-start
  7.4 0.6 copy-start.1

commit v5 on v4

--- a/solution.py
+++ b/solution.py
@@ -137,7 +137,7 @@
     ww[0:128, :] = w_hi
     ww[128:256, :] = (w - w_hi.astype(F32)).astype(BF16)
 
-    def strip(c, mags):
+    def strip(c):
         y0 = pl.multiple_of(c * 16, 16)
         before = pl.multiple_of(jnp.maximum(y0 - 8, 0), 8)
         after = pl.multiple_of(jnp.minimum(y0 + 16, 248), 8)
@@ -154,34 +154,28 @@
             for k in range(21):
                 g[k, gx - 1] = out[k]
             if 2 <= gx <= 5:
-                mags(c, gx - 2, mag)
+                keep(c, gx - 2, mag)
         for k in range(21):
             gs = [g[k, t] for t in range(6)]
             pairs = [gs[t] + gs[t + 1] for t in range(5)]
             for x in range(4):
                 total = pairs[x] + pairs[x + 1]
-                total = total + pltpu.roll(total, 2, 1)
-                box = total + pltpu.roll(total, 126, 1)
+                box = (pltpu.roll(total, 2, 1) + pltpu.roll(total, 126, 1)) + (total + total)
                 hi = box.astype(BF16)
                 bh[k, pl.ds(y0, 16), pl.ds(x * 128, 128)] = hi
                 bl[k, pl.ds(y0, 16), pl.ds(x * 128, 128)] = (box - hi.astype(F32)).astype(BF16)
 
     def keep(c, x, mag):
-        block = 2 * c - 16 * h
+        block = jnp.where(c // 8 == h, 2 * c - 16 * h, 16)
         leo[block, x, 6] = mag[:8]
         leo[block + 1, x, 6] = mag[8:]
 
-    def keep_own(c, x, mag):
-        @pl.when(c // 8 == h)
-        def _():
-            keep(jnp.clip(c, 8 * h, 8 * h + 7), x, mag)
-
     def early(t, _):
-        strip(9 * h + t, keep)
+        strip(9 * h + t)
         return 0
 
     def late(t, _):
-        strip(7 * other + t, keep_own)
+        strip(7 * other + t)
         return 0
 
     across(0).wait_recv()
@@ -376,7 +370,7 @@
             VMEM((21, 128, 256), F32),
             VMEM((256, 256), BF16),
             VMEM((2, 256, 128), jnp.int32),
-            VMEM((16, 4, 7, 8, 128), F32),
+            VMEM((18, 4, 7, 8, 128), F32),
             VMEM((8, 128), F32),
             VMEM((32, 8, 128), F32),
             VMEM((8, 8, 128), F32),

time: 169 us -> 113 us (0.67)
  the two profiles are of different devices: /device:TPU:32 before, /device:TPU:1 now
where the time goes in v5:
time: 113 us; the launch traced here: 112 us
  Pallas kernels  105 us (93%)
  waiting for transfers between devices  3.27 us (3%)
  starting transfers between devices  3.2 us (3%)
    pallas_call x1, Pallas kernels, local_step(): pl.pallas_call(core, out_shape=(jax.ShapeDtypeStruct((16, 4, 7, 8, 128),...  96.5 us
    pallas_call x1, Pallas kernels, local_step(): pl.pallas_call(to_planes, out_shape=(jax.ShapeDtypeStruct((6, 8, 64, 128)...  4.94 us
    pallas_call x1, Pallas kernels, local_step(): pl.pallas_call(to_columns, out_shape=(jax.ShapeDtypeStruct((68 * 24, 128)...  3.31 us
    ppermute x1, starting transfers between devices, local_step(): below = lax.ppermute(right, 'px', [(i, (i + 1) % 8) for i in range(8)])  3.02 us
    ppermute x1, waiting for transfers between devices, local_step(): above = lax.ppermute(left, 'px', [((i + 1) % 8, i) for i in range(8)])  2.3 us
  transfers between devices with their start and end apart: 2, of which 2 were waited for; matrix products, arithmetic and copies ran while one was open for 0% of the time, Pallas kernels for 0%

profile of v5, /device:TPU:1, one launch (start us, length us, event | category | flops | bytes accessed | tf_op | source)
XLA Modules:
  0.0 112.5 jit_solution(4346066613516891752)
XLA Ops:
  0.6 3.3 %to_columns.1 = (f32[1632,128]{1,0:T(8,128)}, f32[48,128]{1,0:T(8,128)}, f32[48,128]{1,0:T(8,128)}) custom-call(f32[3,8,64,128]{3,2,1,0:T(8,128)} %vel_ref.1), custom_call_target="tpu_custom_call" | custom-call | tf_op jit(solution)/shard_map/to_columns/pallas_call | solution.py:342
  3.9 3.0 %collective-permute-start = (f32[48,128]{1,0:T(8,128)}, f32[48,128]{1,0:T(8,128)S(1)}, u32[]{:S(2)}, u32[]{:S(2)}) collective-permute-start(f32[48,128]{1,0:T(8,128)} %get-tuple-element.12), channel_id=1, source_target_pairs={{0,32},{32,64},{64,96},{96,128},{128,160},{160,192},{192,224},{224... | collective-permute-start | bytes 73736 | tf_op jit(solution)/shard_map/ppermute | solution.py:351
  7.0 0.2 collective-permute-start.1
  7.1 1.0 collective-permute-done
  8.1 0.0 copy-start
  8.1 2.3 %collective-permute-done.1 = f32[48,128]{1,0:T(8,128)S(1)} collective-permute-done((f32[48,128]{1,0:T(8,128)}, f32[48,128]{1,0:T(8,128)S(1)}, u32[]{:S(2)}, u32[]{:S(2)}) %collective-permute-start.1) | collective-permute-done | bytes 24608 | tf_op jit(solution)/shard_map/ppermute | solution.py:352
  10.4 0.0 copy-start.1
  10.4 0.0 copy-done
  10.4 0.6 copy-done.1
  11.0 96.5 %core.1 = (f32[16,4,7,8,128]{4,3,2,1,0:T(8,128)}, f32[8,128]{1,0:T(8,128)}) custom-call(f32[68,3,8,128]{3,2,1,0:T(8,128)} %bitcast.8, f32[2,3,8,128]{3,2,1,0:T(8,128)} %bitcast.9, f32[2,3,8,128]{3,2,1,0:T(8,128)} %bitcast.10, f32[256,256]{1,0:T(8,128)} %inv_ref.1, s32[1,256]{1,0:T(1,128)} %bitcast.13, s32[1,256]{1,0:T(1,128)} %bitcast.11), custom_call_target="tpu_custom_call" | custom-call | tf_op jit(solution)/shard_map/core/pallas_call | solution.py:355
  107.5 4.9 %to_planes.1 = (f32[6,8,64,128]{3,2,1,0:T(8,128)}, f32[8,64,128]{2,1,0:T(8,128)}, f32[1,256]{1,0:T(1,128)}) custom-call(f32[8,128]{1,0:T(8,128)} %get-tuple-element.14.tot_ref, s32[1,256]{1,0:T(1,128)} %bitcast.12, f32[3584,128]{1,0:T(8,128)} %bitcast.7), custom_call_target="tpu_custom_call" | custom-call | tf_op jit(solution)/shard_map/to_planes/pallas_call | solution.py:402
Async XLA Ops:
  3.9 4.2 %collective-permute-start = (f32[48,128]{1,0:T(8,128)}, f32[48,128]{1,0:T(8,128)S(1)}, u32[]{:S(2)}, u32[]{:S(2)}) collective-permute-start(f32[48,128]{1,0:T(8,128)} %get-tuple-element.12), channel_id=1, source_target_pairs={{0,32},{32,64},{64,96},{96,128},{128,160},{160,192},{192,224},{224... | collective-permute-start | bytes 73736 | tf_op jit(solution)/shard_map/ppermute | solution.py:351
  7.0 3.5 %collective-permute-start.1 = (f32[48,128]{1,0:T(8,128)}, f32[48,128]{1,0:T(8,128)S(1)}, u32[]{:S(2)}, u32[]{:S(2)}) collective-permute-start(f32[48,128]{1,0:T(8,128)} %get-tuple-element.13), channel_id=1, source_target_pairs={{32,0},{64,32},{96,64},{128,96},{160,128},{192,160},{224,192},{0,2... | collective-permute-start | bytes 73736 | tf_op jit(solution)/shard_map/ppermute | solution.py:352
  8.1 2.3 %copy-start = (f32[48,128]{1,0:T(8,128)}, f32[48,128]{1,0:T(8,128)S(1)}, u32[]{:S(2)}) copy-start(f32[48,128]{1,0:T(8,128)S(1)} %collective-permute-done) | copy-start | bytes 73732
  10.4 0.6 copy-start.1

commit v6 on v5

--- a/solution.py
+++ b/solution.py
@@ -12,8 +12,68 @@
 F32 = jnp.float32
 BF16 = jnp.bfloat16
 VMEM = pltpu.VMEM
-def to_columns(vel_ref, x_ref, right_ref, left_ref, mix):
-    even = lax.broadcasted_iota(jnp.int32, (64, 128), 1) % 2 == 0
+ORDER = (10, 6, 14, 8, 9, 11, 2, 5, 15, 13, 7, 1, 3, 4, 12)
+
+
+def where_am_i():
+    px, pz = lax.axis_index("px"), lax.axis_index("pz")
+    return px, pz, pz // 16, (pz % 16) // 4, pz % 4
+
+
+def fields_of(u, gx, up, down):
+    def d_x(f):
+        return u[f][gx + 1] - u[f][gx - 1]
+
+    def d_z(f):
+        return pltpu.roll(u[f][gx], 126, 1) - pltpu.roll(u[f][gx], 2, 1)
+
+    def d_y(f):
+        return up[f] - down[f]
+
+    t = [d_x(0), d_y(1), d_z(2), d_y(0) + d_x(1), d_z(0) + d_x(2), d_z(1) + d_y(2)]
+    mag = twice_norm(t)
+    a, b, c = u[0][gx], u[1][gx], u[2][gx]
+    return [a, b, c] + t + [a * a, b * b, c * c, a * b, a * c, b * c] + [mag * q for q in t], mag
+
+
+def twice_norm(t):
+    return jnp.sqrt(
+        2.0 * (t[0] * t[0] + t[1] * t[1] + t[2] * t[2]) + (t[3] * t[3] + t[4] * t[4] + t[5] * t[5])
+    )
+
+
+def column(row):
+    return jnp.broadcast_to(row, (128, 256)).T
+
+
+def core(
+    vel_ref, inv_ref, fb_ref, pb_ref, o_ref, tot_ref,
+    rows, partner, edge, near, mix, r, g, bh, bl, ff, ww, bins, leo, part, a1, a2, s1,
+    send_a, recv_a, send_b, recv_b, send_c, recv_c, ss0, rs0, ss1, rs1, ss2, rs2, sb, rb, local,
+):
+    px, pz, h, yy, xx = where_am_i()
+    i = pz % 16
+    other = 1 - h
+
+    def mate(k):
+        return ((yy + k // 4) % 4) * 4 + (xx + k % 4) % 4
+
+    def twin(k):
+        return (px + k % 8) % 8, ((h + k // 8) % 2) * 16 + i
+
+    def send(src, dst, sems, recvs, where):
+        return pltpu.make_async_remote_copy(
+            src_ref=src, dst_ref=dst, send_sem=sems, recv_sem=recvs, device_id=where, device_id_type=MESH
+        )
+
+    barrier = pltpu.get_barrier_semaphore()
+    for k in range(1, 16):
+        pl.semaphore_signal(barrier, inc=1, device_id=(px, h * 16 + mate(k)), device_id_type=MESH)
+        pl.semaphore_signal(barrier, inc=1, device_id=twin(k), device_id_type=MESH)
+
+    flat = rows.reshape(68 * 24, 128)
+    lane = lax.broadcasted_iota(jnp.int32, (64, 128), 1)
+    even = lane % 2 == 0
 
     def plane(y, _):
         for f in range(3):
@@ -21,89 +81,31 @@
             mix[f, pl.ds(0, 64, stride=2), :] = v
             mix[f, pl.ds(1, 64, stride=2), :] = v
             t = mix[f].T
-            x_ref[pl.ds(48 + f * 8 + y, 64, stride=24), :] = jnp.where(even, t[:64], t[64:])
+            flat[pl.ds(48 + f * 8 + y, 64, stride=24), :] = jnp.where(even, t[:64], t[64:])
         return 0
 
     lax.fori_loop(0, 8, plane, 0)
-    first, last = x_ref[48:96, :], x_ref[64 * 24 : 66 * 24, :]
-    x_ref[0:48, :] = pltpu.roll(last, 1, 1)
-    x_ref[66 * 24 : 68 * 24, :] = pltpu.roll(first, 127, 1)
-    right_ref[...] = pltpu.roll(last, 127, 1)
-    left_ref[...] = pltpu.roll(first, 1, 1)
-
-
-ORDER = (10, 6, 14, 8, 9, 11, 2, 5, 15, 13, 7, 1, 3, 4, 12)
-
-
-def where_am_i():
-    px, pz = lax.axis_index("px"), lax.axis_index("pz")
-    return px, pz, pz // 16, (pz % 16) // 4, pz % 4
-
-
-def fields_of(u, gx, up, down):
-    def d_x(f):
-        return u[f][gx + 1] - u[f][gx - 1]
-
-    def d_z(f):
-        return pltpu.roll(u[f][gx], 126, 1) - pltpu.roll(u[f][gx], 2, 1)
-
-    def d_y(f):
-        return up[f] - down[f]
-
-    t = [d_x(0), d_y(1), d_z(2), d_y(0) + d_x(1), d_z(0) + d_x(2), d_z(1) + d_y(2)]
-    mag = twice_norm(t)
-    a, b, c = u[0][gx], u[1][gx], u[2][gx]
-    return [a, b, c] + t + [a * a, b * b, c * c, a * b, a * c, b * c] + [mag * q for q in t], mag
-
-
-def twice_norm(t):
-    return jnp.sqrt(
-        2.0 * (t[0] * t[0] + t[1] * t[1] + t[2] * t[2]) + (t[3] * t[3] + t[4] * t[4] + t[5] * t[5])
-    )
-
-
-def column(row):
-    return jnp.broadcast_to(row, (128, 256)).T
-
-
-def core(
-    x_ref, below_ref, above_ref, inv_ref, fb_ref, pb_ref, o_ref, tot_ref,
-    rows, partner, r, g, bh, bl, ff, ww, bins, leo, part, a1, a2, s1,
-    send_a, recv_a, send_b, recv_b, send_c, recv_c, ss1, rs1, ss2, rs2, sb, rb, local,
-):
-    px, pz, h, yy, xx = where_am_i()
-    i = pz % 16
-    other = 1 - h
-
-    def mate(k):
-        return ((yy + k // 4) % 4) * 4 + (xx + k % 4) % 4
-
-    def peer(k):
-        return ((h + k // 16) % 2) * 16 + mate(k % 16)
-
-    def send(src, dst, sems, recvs, where):
-        return pltpu.make_async_remote_copy(
-            src_ref=src, dst_ref=dst, send_sem=sems, recv_sem=recvs, device_id=where, device_id_type=MESH
-        )
-
-    fetch = pltpu.make_async_copy(x_ref, rows, local.at[0])
-    fetch.start()
-    barrier = pltpu.get_barrier_semaphore()
-    for k in range(1, 32):
-        pl.semaphore_signal(barrier, inc=1, device_id=(px, peer(k)), device_id_type=MESH)
-    for k in range(1, 8):
-        pl.semaphore_signal(barrier, inc=1, device_id=((px + k) % 8, pz), device_id_type=MESH)
-    fetch.wait()
-    even = lax.broadcasted_iota(jnp.int32, (2, 3, 8, 128), 3) % 2 == 0
-    rows[0:2] = jnp.where(even, below_ref[...], rows[0:2])
-    rows[66:68] = jnp.where(even, rows[66:68], above_ref[...])
-    pl.semaphore_wait(barrier, 38)
+    first, last = flat[48:96, :], flat[64 * 24 : 66 * 24, :]
+    edge[0] = pltpu.roll(last, 127, 1)
+    edge[1] = pltpu.roll(first, 1, 1)
+    pl.semaphore_wait(barrier, 30)
 
     own_planes = pl.ds(pl.multiple_of(pz * 8, 8), 8)
     their_planes = pl.ds(pl.multiple_of((other * 16 + i) * 8, 8), 8)
 
-    def across(f):
-        return send(rows.at[:, f], partner.at[:, f], send_a.at[f], recv_a.at[f], (px, other * 16 + i))
+    def across(n):
+        piece = (
+            (pl.ds(2, 64), 0),
+            (pl.ds(2, 64), 1),
+            (pl.ds(2, 40), 2),
+            (pl.ds(42, 24), 2),
+            (pl.ds(0, 2), slice(None)),
+            (pl.ds(66, 2), slice(None)),
+        )[n]
+        return send(rows.at[piece], partner.at[piece], send_a.at[n], recv_a.at[n], (px, other * 16 + i))
+
+    def sideways(n):
+        return send(edge.at[n], near.at[n], ss0.at[n], rs0.at[n], ((px + (1, 7)[n]) % 8, pz))
 
     def own(k):
         return send(
@@ -120,12 +122,20 @@
     def there(f):
         return pltpu.make_async_copy(partner.at[pl.ds(i * 4, 8), f], r.at[:, f, their_planes, :], local.at[1 + f])
 
-    for f in range(3):
-        across(f).start()
-    for k in ORDER:
-        own(k).start()
-    here = pltpu.make_async_copy(rows.at[pl.ds(i * 4, 8)], r.at[:, :, own_planes, :], local.at[0])
-    here.start()
+    sideways(0).start()
+    sideways(1).start()
+    across(0).start()
+    for k in ORDER:
+
+        @pl.when(mate(k) % 15 != 0)
+        def _(k=k):
+            own(k).start()
+
+    sideways(0).wait_recv()
+    sideways(1).wait_recv()
+    even = lax.broadcasted_iota(jnp.int32, (48, 128), 1) % 2 == 0
+    flat[0:48, :] = jnp.where(even, near[0], pltpu.roll(last, 1, 1))
+    flat[66 * 24 : 68 * 24, :] = jnp.where(even, pltpu.roll(first, 127, 1), near[1])
 
     r0 = pl.multiple_of(h * 128, 128)
     bins[0] = column(fb_ref[...])
@@ -136,6 +146,17 @@
     w_hi = w.astype(BF16)
     ww[0:128, :] = w_hi
     ww[128:256, :] = (w - w_hi.astype(F32)).astype(BF16)
+
+    for n in (4, 5, 1, 2, 3):
+        across(n).start()
+    for k in ORDER:
+
+        @pl.when(mate(k) % 15 == 0)
+        def _(k=k):
+            own(k).start()
+
+    here = pltpu.make_async_copy(rows.at[pl.ds(i * 4, 8)], r.at[:, :, own_planes, :], local.at[0])
+    here.start()
 
     def strip(c):
         y0 = pl.multiple_of(c * 16, 16)
@@ -179,6 +200,8 @@
         return 0
 
     across(0).wait_recv()
+    across(4).wait_recv()
+    across(5).wait_recv()
     for k in ORDER:
         theirs(0, k).start()
     there(0).start()
@@ -186,11 +209,25 @@
     for k in range(1, 16):
         own(k).wait_recv()
     lax.fori_loop(0, 7, early, 0)
-    for f in (1, 2):
-        across(f).wait_recv()
-        for k in ORDER:
-            theirs(f, k).start()
-        there(f).start()
+    across(1).wait_recv()
+    for k in ORDER:
+        theirs(1, k).start()
+    there(1).start()
+    across(2).wait_recv()
+    for k in ORDER:
+
+        @pl.when(mate(k) <= 8)
+        def _(k=k):
+            theirs(2, k).start()
+
+    across(3).wait_recv()
+    for k in ORDER:
+
+        @pl.when(mate(k) > 8)
+        def _(k=k):
+            theirs(2, k).start()
+
+    there(2).start()
     for f in range(3):
         there(f).wait()
         for k in range(1, 16):
@@ -199,7 +236,7 @@
 
     lanes = lax.broadcasted_iota(jnp.int32, (8, 128), 1)
 
-    def products(x0):
+    def products(x0, start, stop):
         def product(q, _):
             for t in range(3):
                 k = q * 3 + t
@@ -210,7 +247,7 @@
                 ff[k] = both[:128] + (both[128:] + rest)
             return 0
 
-        lax.fori_loop(0, 7, product, 0)
+        lax.fori_loop(start, stop, product, 0)
 
     def contracts(x0, sums):
         def contract(c, sums):
@@ -245,55 +282,60 @@
         )
 
     def small(k):
-        return send(part, a1.at[pz], ss1.at[k], rs1.at[k], (px, peer(k)))
+        return send(part, a1.at[h * 8 + px], ss1.at[k], rs1.at[k], twin(k))
 
     def second(k):
-        return send(s1, a2.at[px], ss2.at[k], rs2.at[k], ((px + k) % 8, pz))
+        return send(s1, a2.at[i], ss2.at[k], rs2.at[k], (px, h * 16 + mate(k)))
 
     zero = jnp.zeros((8, 128), F32)
-    products(0)
+    products(0, 0, 7)
     sums = contracts(0, (zero, zero))
-    products(2)
+    products(2, 0, 1)
     for k in ORDER:
         big(0, k).start()
+    products(2, 1, 7)
     num, den = contracts(2, sums)
     row = lax.broadcasted_iota(jnp.int32, (8, 128), 0)
     num = jnp.sum(num, axis=0, keepdims=True) * 0.25
     den = jnp.sum(den, axis=0, keepdims=True) * 0.03125
     mine = jnp.where(row == 0, num, jnp.where(row == 1, den, 0.0))
     part[...] = mine
-    a1[pz] = mine
-    for f in range(3):
-        across(f).wait_send()
-        for k in range(1, 16):
+    a1[h * 8 + px] = mine
+    for n in range(6):
+        across(n).wait_send()
+    for n in range(2):
+        sideways(n).wait_send()
+    for k in range(1, 16):
+        own(k).wait_send()
+        for f in range(3):
             theirs(f, k).wait_send()
     for k in range(1, 16):
-        own(k).wait_send()
-    for k in range(1, 32):
         small(k).start()
-    for k in ORDER:
+    for k in ORDER[:6]:
         big(1, k).start()
     keep_here = pltpu.make_async_copy(leo.at[i], o_ref.at[i], local.at[0])
     keep_here.start()
-    for k in range(1, 32):
+    for k in range(1, 16):
         small(k).wait_recv()
     total = a1[0]
-    for q in range(1, 32):
+    for q in range(1, 16):
         total = total + a1[q]
     s1[...] = total
-    a2[px] = total
-    for k in range(1, 32):
+    a2[i] = total
+    for k in range(1, 16):
         small(k).wait_send()
-    for k in range(1, 8):
+    for k in range(1, 16):
         second(k).start()
-    for k in range(1, 8):
+    for k in ORDER[6:]:
+        big(1, k).start()
+    for k in range(1, 16):
         second(k).wait_recv()
     total = a2[0]
-    for q in range(1, 8):
+    for q in range(1, 16):
         total = total + a2[q]
     tot_ref[...] = total
     keep_here.wait()
-    for k in range(1, 8):
+    for k in range(1, 16):
         second(k).wait_send()
     for half in range(2):
         for k in range(1, 16):
@@ -338,18 +380,6 @@
 
 
 def local_step(velocity, filter_inverse, filter_block, plane_bin):
-    edge = jax.ShapeDtypeStruct((48, 128), F32)
-    rows, right, left = pl.pallas_call(
-        to_columns,
-        out_shape=(jax.ShapeDtypeStruct((68 * 24, 128), F32), edge, edge),
-        in_specs=[spec(VMEM)],
-        out_specs=(spec(VMEM),) * 3,
-        scratch_shapes=[VMEM((3, 128, 128), F32)],
-        compiler_params=params(),
-        name="to_columns",
-    )(velocity)
-    below = lax.ppermute(right, "px", [(i, (i + 1) % 8) for i in range(8)])
-    above = lax.ppermute(left, "px", [((i + 1) % 8, i) for i in range(8)])
     bins = plane_bin.reshape(1, 256)
     part = VMEM((68, 3, 8, 128), F32)
     back, total = pl.pallas_call(
@@ -358,11 +388,14 @@
             jax.ShapeDtypeStruct((16, 4, 7, 8, 128), F32),
             jax.ShapeDtypeStruct((8, 128), F32),
         ),
-        in_specs=[spec(pl.ANY)] + [spec(VMEM)] * 5,
+        in_specs=[spec(VMEM)] * 4,
         out_specs=(spec(pl.ANY), spec(VMEM)),
         scratch_shapes=[
             part,
             part,
+            VMEM((2, 48, 128), F32),
+            VMEM((2, 48, 128), F32),
+            VMEM((3, 128, 128), F32),
             VMEM((8, 3, 256, 128), F32),
             VMEM((21, 6, 16, 128), F32),
             VMEM((21, 256, 512), BF16),
@@ -372,19 +405,21 @@
             VMEM((2, 256, 128), jnp.int32),
             VMEM((18, 4, 7, 8, 128), F32),
             VMEM((8, 128), F32),
-            VMEM((32, 8, 128), F32),
-            VMEM((8, 8, 128), F32),
+            VMEM((16, 8, 128), F32),
+            VMEM((16, 8, 128), F32),
             VMEM((8, 128), F32),
-            DMA((3,)),
-            DMA((3,)),
+            DMA((6,)),
+            DMA((6,)),
             DMA((16,)),
             DMA((16,)),
             DMA((3, 16)),
             DMA((3, 16)),
-            DMA((32,)),
-            DMA((32,)),
-            DMA((8,)),
-            DMA((8,)),
+            DMA((2,)),
+            DMA((2,)),
+            DMA((16,)),
+            DMA((16,)),
+            DMA((16,)),
+            DMA((16,)),
             DMA((2, 16)),
             DMA((2, 16)),
             DMA((4,)),
@@ -392,9 +427,7 @@
         compiler_params=params(collective_id=0, has_side_effects=True),
         name="core",
     )(
-        rows.reshape(68, 3, 8, 128),
-        below.reshape(2, 3, 8, 128),
-        above.reshape(2, 3, 8, 128),
+        velocity,
         filter_inverse,
         filter_block.reshape(1, 256),
         bins,

time: 113 us -> 97.1 us (0.86)
  the two profiles are of different devices: /device:TPU:1 before, /device:TPU:32 now
where the time goes in v6:
time: 97.1 us; the launch traced here: 96.7 us
  Pallas kernels  96.1 us (99%)
    pallas_call x1, Pallas kernels, local_step(): pl.pallas_call(core, out_shape=(jax.ShapeDtypeStruct((16, 4, 7, 8, 128),...  91.1 us
    pallas_call x1, Pallas kernels, local_step(): pl.pallas_call(to_planes, out_shape=(jax.ShapeDtypeStruct((6, 8, 64, 128)...  4.94 us

profile of v6, /device:TPU:32, one launch (start us, length us, event | category | flops | bytes accessed | tf_op | source)
XLA Modules:
  0.0 96.7 jit_solution(2640533761422828476)
XLA Ops:
  0.6 91.1 %core.1 = (f32[16,4,7,8,128]{4,3,2,1,0:T(8,128)}, f32[8,128]{1,0:T(8,128)}) custom-call(f32[3,8,64,128]{3,2,1,0:T(8,128)} %vel_ref.1, f32[256,256]{1,0:T(8,128)} %inv_ref.1, s32[1,256]{1,0:T(1,128)} %bitcast.7, s32[1,256]{1,0:T(1,128)} %bitcast.5), custom_call_target="tpu_custom_call" | custom-call | tf_op jit(solution)/shard_map/core/pallas_call | solution.py:385
  91.8 4.9 %to_planes.1 = (f32[6,8,64,128]{3,2,1,0:T(8,128)}, f32[8,64,128]{2,1,0:T(8,128)}, f32[1,256]{1,0:T(1,128)}) custom-call(f32[8,128]{1,0:T(8,128)} %get-tuple-element.8.tot_ref, s32[1,256]{1,0:T(1,128)} %bitcast.6, f32[3584,128]{1,0:T(8,128)} %bitcast.4), custom_call_target="tpu_custom_call" | custom-call | tf_op jit(solution)/shard_map/to_planes/pallas_call | solution.py:435

commit v7 on v6

--- a/solution.py
+++ b/solution.py
@@ -20,6 +20,10 @@
     return px, pz, pz // 16, (pz % 16) // 4, pz % 4
 
 
+SLOT = (0, 1, 8, 2, 3, 9, 4, 10, 11, 5, 6, 12, 7, 13, 14, 15, 16, 17, 18, 19, 20)
+EARLY = 8
+
+
 def fields_of(u, gx, up, down):
     def d_x(f):
         return u[f][gx + 1] - u[f][gx - 1]
@@ -47,9 +51,9 @@
 
 
 def core(
-    vel_ref, inv_ref, fb_ref, pb_ref, o_ref, tot_ref,
-    rows, partner, edge, near, mix, r, g, bh, bl, ff, ww, bins, leo, part, a1, a2, s1,
-    send_a, recv_a, send_b, recv_b, send_c, recv_c, ss0, rs0, ss1, rs1, ss2, rs2, sb, rb, local,
+    vel_ref, inv_ref, fb_ref, pb_ref, o_ref, om_ref, tot_ref,
+    rows, partner, edge, near, mix, r, g, bh, bl, ff, ww, bins, leo, mg, part, a1, a2, s1,
+    send_a, recv_a, send_b, recv_b, send_c, recv_c, ss0, rs0, ss1, rs1, ss2, rs2, sb, rb, sm, rm, local,
 ):
     px, pz, h, yy, xx = where_am_i()
     i = pz % 16
@@ -158,7 +162,7 @@
     here = pltpu.make_async_copy(rows.at[pl.ds(i * 4, 8)], r.at[:, :, own_planes, :], local.at[0])
     here.start()
 
-    def strip(c):
+    def strip(c, slots):
         y0 = pl.multiple_of(c * 16, 16)
         before = pl.multiple_of(jnp.maximum(y0 - 8, 0), 8)
         after = pl.multiple_of(jnp.minimum(y0 + 16, 248), 8)
@@ -173,10 +177,11 @@
                 up.append(jnp.concatenate([u[f][gx][1:], succ[:1]], axis=0))
             out, mag = fields_of(u, gx, up, down)
             for k in range(21):
-                g[k, gx - 1] = out[k]
-            if 2 <= gx <= 5:
+                if SLOT[k] in slots:
+                    g[SLOT[k], gx - 1] = out[k]
+            if 2 <= gx <= 5 and 20 in slots:
                 keep(c, gx - 2, mag)
-        for k in range(21):
+        for k in slots:
             gs = [g[k, t] for t in range(6)]
             pairs = [gs[t] + gs[t + 1] for t in range(5)]
             for x in range(4):
@@ -188,16 +193,31 @@
 
     def keep(c, x, mag):
         block = jnp.where(c // 8 == h, 2 * c - 16 * h, 16)
-        leo[block, x, 6] = mag[:8]
-        leo[block + 1, x, 6] = mag[8:]
+        mg[block, x] = mag[:8]
+        mg[block + 1, x] = mag[8:]
 
     def early(t, _):
-        strip(9 * h + t)
+        strip(9 * h + t, range(21))
         return 0
 
-    def late(t, _):
-        strip(7 * other + t)
+    def late_a(t, _):
+        strip(7 * other + t, range(EARLY))
         return 0
+
+    def late_b(t, _):
+        strip(7 * other + t, range(EARLY, 21))
+        return 0
+
+    def products(half, slots):
+        for k in slots:
+            hi = bh[k, :, pl.ds(half * 256, 256)]
+            lo = bl[k, :, pl.ds(half * 256, 256)]
+            both = jnp.dot(ww[...], hi, preferred_element_type=F32)
+            rest = jnp.dot(ww[0:128, :], lo, preferred_element_type=F32)
+            ff[half, k] = both[:128] + (both[128:] + rest)
+
+    def lengths(k):
+        return send(mg.at[mate(k)], om_ref.at[i], sm.at[k], rm.at[k], (px, h * 16 + mate(k)))
 
     across(0).wait_recv()
     across(4).wait_recv()
@@ -213,6 +233,12 @@
     for k in ORDER:
         theirs(1, k).start()
     there(1).start()
+    for k in ORDER:
+
+        @pl.when(mate(k) // 2 != 7 * other)
+        def _(k=k):
+            lengths(k).start()
+
     across(2).wait_recv()
     for k in ORDER:
 
@@ -228,33 +254,26 @@
             theirs(2, k).start()
 
     there(2).start()
-    for f in range(3):
+    for f in range(2):
         there(f).wait()
         for k in range(1, 16):
             theirs(f, k).wait_recv()
-    lax.fori_loop(0, 9, late, 0)
+    lax.fori_loop(0, 9, late_a, 0)
+    products(0, range(EARLY))
+    products(1, range(EARLY))
+    there(2).wait()
+    for k in range(1, 16):
+        theirs(2, k).wait_recv()
+    lax.fori_loop(0, 9, late_b, 0)
 
     lanes = lax.broadcasted_iota(jnp.int32, (8, 128), 1)
-
-    def products(x0, start, stop):
-        def product(q, _):
-            for t in range(3):
-                k = q * 3 + t
-                hi = bh[k, :, pl.ds(x0 * 128, 256)]
-                lo = bl[k, :, pl.ds(x0 * 128, 256)]
-                both = jnp.dot(ww[...], hi, preferred_element_type=F32)
-                rest = jnp.dot(ww[0:128, :], lo, preferred_element_type=F32)
-                ff[k] = both[:128] + (both[128:] + rest)
-            return 0
-
-        lax.fori_loop(start, stop, product, 0)
 
     def contracts(x0, sums):
         def contract(c, sums):
             y0 = pl.multiple_of(c * 8, 8)
             lm_sum, mm_sum = 0.0, 0.0
             for x in range(2):
-                f = [ff[k, pl.ds(y0, 8), pl.ds(x * 128, 128)] for k in range(21)]
+                f = [ff[x0 // 2, SLOT[k], pl.ds(y0, 8), pl.ds(x * 128, 128)] for k in range(21)]
                 a, b, d = f[0], f[1], f[2]
                 t, p, m = f[3:9], f[9:15], f[15:21]
                 uu = [a * a, b * b, d * d, a * b, a * d, b * d]
@@ -288,12 +307,18 @@
         return send(s1, a2.at[i], ss2.at[k], rs2.at[k], (px, h * 16 + mate(k)))
 
     zero = jnp.zeros((8, 128), F32)
-    products(0, 0, 7)
+    products(0, range(EARLY, 21))
     sums = contracts(0, (zero, zero))
-    products(2, 0, 1)
+    products(1, range(EARLY, EARLY + 4))
+    for k in ORDER:
+
+        @pl.when(mate(k) // 2 == 7 * other)
+        def _(k=k):
+            lengths(k).start()
+
     for k in ORDER:
         big(0, k).start()
-    products(2, 1, 7)
+    products(1, range(EARLY + 4, 21))
     num, den = contracts(2, sums)
     row = lax.broadcasted_iota(jnp.int32, (8, 128), 0)
     num = jnp.sum(num, axis=0, keepdims=True) * 0.25
@@ -315,6 +340,8 @@
         big(1, k).start()
     keep_here = pltpu.make_async_copy(leo.at[i], o_ref.at[i], local.at[0])
     keep_here.start()
+    keep_length = pltpu.make_async_copy(mg.at[i], om_ref.at[i], local.at[1])
+    keep_length.start()
     for k in range(1, 16):
         small(k).wait_recv()
     total = a1[0]
@@ -335,14 +362,16 @@
         total = total + a2[q]
     tot_ref[...] = total
     keep_here.wait()
+    keep_length.wait()
     for k in range(1, 16):
         second(k).wait_send()
+        lengths(k).wait()
     for half in range(2):
         for k in range(1, 16):
             big(half, k).wait()
 
 
-def to_planes(tot_ref, pb_ref, o_ref, leo_ref, visc_ref, coef_ref, mix):
+def to_planes(tot_ref, pb_ref, o_ref, om_ref, leo_ref, visc_ref, coef_ref, mix):
     pz = lax.axis_index("pz")
     per_bin = tot_ref[0:1, :] / jnp.maximum(tot_ref[1:2, :], 65536.0)
     per_bin = jnp.broadcast_to(per_bin, (128, 128)).T
@@ -352,20 +381,25 @@
     coef_ref[...] = coef
     at = lax.broadcasted_iota(jnp.int32, (1, 256), 1) - pz * 8
     low = lax.broadcasted_iota(jnp.int32, (64, 128), 1) < 64
-
-    def plane(y, _):
+    y0 = pl.program_id(0) * 4
+
+    def plane(t, _):
+        y = y0 + t
         mine = jnp.sum(jnp.where(at == y, coef, 0.0), axis=1, keepdims=True)
         for f in range(7):
-            m = o_ref[pl.ds(f * 8 + y, 64, stride=56), :]
+            if f < 6:
+                m = o_ref[pl.ds(f * 8 + y, 64, stride=48), :]
+            else:
+                m = om_ref[pl.ds(y, 64, stride=8), :]
             mix[f] = jnp.concatenate([m, m], axis=0).T
             v = jnp.where(low, mix[f, pl.ds(0, 64, stride=2), :], mix[f, pl.ds(1, 64, stride=2), :])
             if f < 6:
-                leo_ref[f, y] = v
+                leo_ref[f, t] = v
             else:
-                visc_ref[y] = mine * 0.5 * v
+                visc_ref[t] = mine * 0.5 * v
         return 0
 
-    lax.fori_loop(0, 8, plane, 0)
+    lax.fori_loop(0, 4, plane, 0)
 
 
 def spec(space):
@@ -382,14 +416,15 @@
 def local_step(velocity, filter_inverse, filter_block, plane_bin):
     bins = plane_bin.reshape(1, 256)
     part = VMEM((68, 3, 8, 128), F32)
-    back, total = pl.pallas_call(
+    back, lengths, total = pl.pallas_call(
         core,
         out_shape=(
-            jax.ShapeDtypeStruct((16, 4, 7, 8, 128), F32),
+            jax.ShapeDtypeStruct((16, 4, 6, 8, 128), F32),
+            jax.ShapeDtypeStruct((16, 4, 8, 128), F32),
             jax.ShapeDtypeStruct((8, 128), F32),
         ),
         in_specs=[spec(VMEM)] * 4,
-        out_specs=(spec(pl.ANY), spec(VMEM)),
+        out_specs=(spec(pl.ANY), spec(pl.ANY), spec(VMEM)),
         scratch_shapes=[
             part,
             part,
@@ -400,10 +435,11 @@
             VMEM((21, 6, 16, 128), F32),
             VMEM((21, 256, 512), BF16),
             VMEM((21, 256, 512), BF16),
-            VMEM((21, 128, 256), F32),
+            VMEM((2, 21, 128, 256), F32),
             VMEM((256, 256), BF16),
             VMEM((2, 256, 128), jnp.int32),
-            VMEM((18, 4, 7, 8, 128), F32),
+            VMEM((16, 4, 6, 8, 128), F32),
+            VMEM((18, 4, 8, 128), F32),
             VMEM((8, 128), F32),
             VMEM((16, 8, 128), F32),
             VMEM((16, 8, 128), F32),
@@ -422,6 +458,8 @@
             DMA((16,)),
             DMA((2, 16)),
             DMA((2, 16)),
+            DMA((16,)),
+            DMA((16,)),
             DMA((4,)),
         ],
         compiler_params=params(collective_id=0, has_side_effects=True),
@@ -439,12 +477,22 @@
             jax.ShapeDtypeStruct((8, 64, 128), F32),
             jax.ShapeDtypeStruct((1, 256), F32),
         ),
-        in_specs=[spec(VMEM)] * 3,
-        out_specs=(spec(VMEM),) * 3,
+        grid=(2,),
+        in_specs=[
+            pl.BlockSpec((8, 128), lambda q: (0, 0)),
+            pl.BlockSpec((1, 256), lambda q: (0, 0)),
+            pl.BlockSpec((64 * 48, 128), lambda q: (0, 0)),
+            pl.BlockSpec((64 * 8, 128), lambda q: (0, 0)),
+        ],
+        out_specs=(
+            pl.BlockSpec((6, 4, 64, 128), lambda q: (0, q, 0, 0)),
+            pl.BlockSpec((4, 64, 128), lambda q: (q, 0, 0)),
+            pl.BlockSpec((1, 256), lambda q: (0, 0)),
+        ),
         scratch_shapes=[VMEM((7, 128, 128), F32)],
         compiler_params=params(),
         name="to_planes",
-    )(total, bins, back.reshape(16 * 4 * 56, 128))
+    )(total, bins, back.reshape(64 * 48, 128), lengths.reshape(64 * 8, 128))
     return leonard, viscosity, coefficient.reshape(256)
 
 

time: 97.1 us -> 95.1 us (0.979)
  Pallas kernels: 96.1 us -> 94.3 us
    pallas_call x1, Pallas kernels: 91.1 us -> 89.5 us  [local_step(): pl.pallas_call(core, out_shape=(jax.ShapeDtypeStruct((16, 4, 6, 8, 128),...]
where the time goes in v7:
time: 95.1 us; the launch traced here: 94.9 us
  Pallas kernels  94.3 us (99%)
    pallas_call x1, Pallas kernels, local_step(): pl.pallas_call(core, out_shape=(jax.ShapeDtypeStruct((16, 4, 6, 8, 128),...  89.5 us
    pallas_call x1, Pallas kernels, local_step(): pl.pallas_call(to_planes, out_shape=(jax.ShapeDtypeStruct((6, 8, 64, 128)...  4.79 us

profile of v7, /device:TPU:32, one launch (start us, length us, event | category | flops | bytes accessed | tf_op | source)
XLA Modules:
  0.0 94.9 jit_solution(644027036789961417)
XLA Ops:
  0.6 89.5 %core.1 = (f32[16,4,6,8,128]{4,3,2,1,0:T(8,128)}, f32[16,4,8,128]{3,2,1,0:T(8,128)}, f32[8,128]{1,0:T(8,128)}) custom-call(f32[3,8,64,128]{3,2,1,0:T(8,128)} %vel_ref.1, f32[256,256]{1,0:T(8,128)} %inv_ref.1, s32[1,256]{1,0:T(1,128)} %bitcast.9, s32[1,256]{1,0:T(1,128)} %bitcast.7), custom_call_target="tpu_custom_call" | custom-call | tf_op jit(solution)/shard_map/core/pallas_call | solution.py:419
  90.1 4.8 %to_planes.1 = (f32[6,8,64,128]{3,2,1,0:T(8,128)}, f32[8,64,128]{2,1,0:T(8,128)}, f32[1,256]{1,0:T(1,128)}) custom-call(f32[8,128]{1,0:T(8,128)} %get-tuple-element.9.tot_ref, s32[1,256]{1,0:T(1,128)} %bitcast.8, f32[3072,128]{1,0:T(8,128)} %bitcast.5, f32[512,128]{1,0:T(8,128)} %bitcast.6), custom_call_target="tpu_custom_call" | custom-call | tf_op jit(solution)/shard_map/to_planes/pallas_call | solution.py:473

commit v8 on v7

--- a/solution.py
+++ b/solution.py
@@ -15,6 +15,9 @@
 ORDER = (10, 6, 14, 8, 9, 11, 2, 5, 15, 13, 7, 1, 3, 4, 12)
 
 
+WINDOWS = (12, 13, 10, 11, 14, 15, 4, 5, 2, 3, 6, 7, 8, 9, 0, 1)
+
+
 def where_am_i():
     px, pz = lax.axis_index("px"), lax.axis_index("pz")
     return px, pz, pz // 16, (pz % 16) // 4, pz % 4
@@ -53,7 +56,7 @@
 def core(
     vel_ref, inv_ref, fb_ref, pb_ref, o_ref, om_ref, tot_ref,
     rows, partner, edge, near, mix, r, g, bh, bl, ff, ww, bins, leo, mg, part, a1, a2, s1,
-    send_a, recv_a, send_b, recv_b, send_c, recv_c, ss0, rs0, ss1, rs1, ss2, rs2, sb, rb, sm, rm, local,
+    send_a, recv_a, send_b, recv_b, send_c, recv_c, ss0, rs0, sw, rw, ss1, rs1, ss2, rs2, sb, rb, sm, rm, local,
 ):
     px, pz, h, yy, xx = where_am_i()
     i = pz % 16
@@ -70,9 +73,43 @@
             src_ref=src, dst_ref=dst, send_sem=sems, recv_sem=recvs, device_id=where, device_id_type=MESH
         )
 
+    core_of = px % 2
+    base = px - core_of
+    mixed = xx % 2 != core_of
+    slot = 2 * (2 * yy + xx // 2) + core_of
+
+    def window(k):
+        y2, x2 = (yy + (k // 2) % 4) % 4, (xx // 2 + k // 8) % 2
+        t = 2 * (2 * y2 + x2) + k % 2
+        return t, (base + k % 2, h * 16 + y2 * 4 + 2 * x2 + core_of)
+
+    def start_of(t):
+        return 8 * (t // 2) + 6 * (t % 2)
+
+    def leaves(k):
+        return jnp.logical_or(mixed, core_of != k)
+
+    def each(ks, act, also=None):
+        for k in ks:
+            keep = None if k > 1 else leaves(k)
+            if also is not None:
+                keep = also(k) if keep is None else jnp.logical_and(keep, also(k))
+            if keep is None:
+                act(k)
+            else:
+                pl.when(keep)(functools.partial(act, k))
+
+    def from_all(act):
+        for q in range(16):
+            pl.when(jnp.logical_or(mixed, i != q))(functools.partial(act, q))
+
     barrier = pltpu.get_barrier_semaphore()
-    for k in range(1, 16):
-        pl.semaphore_signal(barrier, inc=1, device_id=(px, h * 16 + mate(k)), device_id_type=MESH)
+    for k in range(16):
+        for c in range(2):
+            if k or c:
+                place = (base + (core_of + c) % 2, h * 16 + mate(k))
+                pl.semaphore_signal(barrier, inc=1, device_id=place, device_id_type=MESH)
+    for k in range(1, 16):
         pl.semaphore_signal(barrier, inc=1, device_id=twin(k), device_id_type=MESH)
 
     flat = rows.reshape(68 * 24, 128)
@@ -92,7 +129,7 @@
     first, last = flat[48:96, :], flat[64 * 24 : 66 * 24, :]
     edge[0] = pltpu.roll(last, 127, 1)
     edge[1] = pltpu.roll(first, 1, 1)
-    pl.semaphore_wait(barrier, 30)
+    pl.semaphore_wait(barrier, 46)
 
     own_planes = pl.ds(pl.multiple_of(pz * 8, 8), 8)
     their_planes = pl.ds(pl.multiple_of((other * 16 + i) * 8, 8), 8)
@@ -111,30 +148,47 @@
     def sideways(n):
         return send(edge.at[n], near.at[n], ss0.at[n], rs0.at[n], ((px + (1, 7)[n]) % 8, pz))
 
-    def own(k):
+    def own(k, q=0):
+        t, place = window(k)
         return send(
-            rows.at[pl.ds(mate(k) * 4, 8)], r.at[:, :, own_planes, :],
-            send_b.at[k], recv_b.at[k], (px, h * 16 + mate(k)),
-        )
-
-    def theirs(f, k):
+            rows.at[pl.ds(start_of(t), 6)], r.at[pl.ds(2 * (k % 2), 6), :, own_planes, :],
+            send_b.at[k], recv_b.at[q], place,
+        )
+
+    def theirs(f, k, q=0):
+        t, place = window(k)
         return send(
-            partner.at[pl.ds(mate(k) * 4, 8), f], r.at[:, f, their_planes, :],
-            send_c.at[f, k], recv_c.at[f, k], (px, h * 16 + mate(k)),
+            partner.at[pl.ds(start_of(t), 6), f], r.at[pl.ds(2 * (k % 2), 6), f, their_planes, :],
+            send_c.at[f, k], recv_c.at[f, q], place,
+        )
+
+    def here():
+        return pltpu.make_async_copy(
+            rows.at[pl.ds(start_of(slot), 6)], r.at[pl.ds(2 * core_of, 6), :, own_planes, :], local.at[0]
         )
 
     def there(f):
-        return pltpu.make_async_copy(partner.at[pl.ds(i * 4, 8), f], r.at[:, f, their_planes, :], local.at[1 + f])
+        return pltpu.make_async_copy(
+            partner.at[pl.ds(start_of(slot), 6), f],
+            r.at[pl.ds(2 * core_of, 6), f, their_planes, :],
+            local.at[1 + f],
+        )
+
+    def swap(n):
+        half = h if n == 0 else other
+        which = (slice(None) if n == 0 else n - 1, pl.ds(pl.multiple_of(half * 128, 128), 128), slice(None))
+        return send(
+            r.at[(pl.ds(4 - 2 * core_of, 2), *which)], r.at[(pl.ds(6 * core_of, 2), *which)],
+            sw.at[n], rw.at[n], (base + 1 - core_of, pz),
+        )
+
+    def alone(act):
+        pl.when(jnp.logical_not(mixed))(act)
 
     sideways(0).start()
     sideways(1).start()
     across(0).start()
-    for k in ORDER:
-
-        @pl.when(mate(k) % 15 != 0)
-        def _(k=k):
-            own(k).start()
-
+    each(WINDOWS, lambda k: own(k, i).start(), lambda k: window(k)[0] % 15 != 0)
     sideways(0).wait_recv()
     sideways(1).wait_recv()
     even = lax.broadcasted_iota(jnp.int32, (48, 128), 1) % 2 == 0
@@ -153,14 +207,8 @@
 
     for n in (4, 5, 1, 2, 3):
         across(n).start()
-    for k in ORDER:
-
-        @pl.when(mate(k) % 15 == 0)
-        def _(k=k):
-            own(k).start()
-
-    here = pltpu.make_async_copy(rows.at[pl.ds(i * 4, 8)], r.at[:, :, own_planes, :], local.at[0])
-    here.start()
+    each(WINDOWS, lambda k: own(k, i).start(), lambda k: window(k)[0] % 15 == 0)
+    alone(lambda: here().start())
 
     def strip(c, slots):
         y0 = pl.multiple_of(c * 16, 16)
@@ -216,54 +264,49 @@
             rest = jnp.dot(ww[0:128, :], lo, preferred_element_type=F32)
             ff[half, k] = both[:128] + (both[128:] + rest)
 
-    def lengths(k):
-        return send(mg.at[mate(k)], om_ref.at[i], sm.at[k], rm.at[k], (px, h * 16 + mate(k)))
+    def owner(k):
+        return (base + xx % 2, h * 16 + mate(k))
+
+    def goes(k):
+        return True if k else mixed
+
+    def lengths(k, t=0):
+        return send(mg.at[mate(k)], om_ref.at[slot], sm.at[k], rm.at[t], owner(k))
 
     across(0).wait_recv()
     across(4).wait_recv()
     across(5).wait_recv()
-    for k in ORDER:
-        theirs(0, k).start()
-    there(0).start()
-    here.wait()
-    for k in range(1, 16):
-        own(k).wait_recv()
+    each(WINDOWS, lambda k: theirs(0, k, i).start())
+    alone(lambda: there(0).start())
+    alone(lambda: here().wait())
+    from_all(lambda q: own(0, q).wait_recv())
+    swap(0).start()
+    swap(0).wait_recv()
     lax.fori_loop(0, 7, early, 0)
     across(1).wait_recv()
-    for k in ORDER:
-        theirs(1, k).start()
-    there(1).start()
-    for k in ORDER:
-
-        @pl.when(mate(k) // 2 != 7 * other)
-        def _(k=k):
-            lengths(k).start()
+    each(WINDOWS, lambda k: theirs(1, k, i).start())
+    alone(lambda: there(1).start())
+    for k in ORDER + (0,):
+        pl.when(jnp.logical_and(goes(k), mate(k) // 2 != 7 * other))(lambda k=k: lengths(k, slot).start())
 
     across(2).wait_recv()
-    for k in ORDER:
-
-        @pl.when(mate(k) <= 8)
-        def _(k=k):
-            theirs(2, k).start()
-
+    each(WINDOWS, lambda k: theirs(2, k, i).start(), lambda k: window(k)[0] <= 8)
     across(3).wait_recv()
-    for k in ORDER:
-
-        @pl.when(mate(k) > 8)
-        def _(k=k):
-            theirs(2, k).start()
-
-    there(2).start()
+    each(WINDOWS, lambda k: theirs(2, k, i).start(), lambda k: window(k)[0] > 8)
+    alone(lambda: there(2).start())
     for f in range(2):
-        there(f).wait()
-        for k in range(1, 16):
-            theirs(f, k).wait_recv()
+        alone(lambda f=f: there(f).wait())
+        from_all(lambda q, f=f: theirs(f, 0, q).wait_recv())
+        swap(1 + f).start()
+    swap(1).wait_recv()
+    swap(2).wait_recv()
     lax.fori_loop(0, 9, late_a, 0)
     products(0, range(EARLY))
     products(1, range(EARLY))
-    there(2).wait()
-    for k in range(1, 16):
-        theirs(2, k).wait_recv()
+    alone(lambda: there(2).wait())
+    from_all(lambda q: theirs(2, 0, q).wait_recv())
+    swap(3).start()
+    swap(3).wait_recv()
     lax.fori_loop(0, 9, late_b, 0)
 
     lanes = lax.broadcasted_iota(jnp.int32, (8, 128), 1)
@@ -294,10 +337,10 @@
 
         return lax.fori_loop(0, 16, contract, sums)
 
-    def big(half, k):
+    def big(half, k, t=0):
         return send(
-            leo.at[mate(k), pl.ds(half * 2, 2)], o_ref.at[i, pl.ds(half * 2, 2)],
-            sb.at[half, k], rb.at[half, k], (px, h * 16 + mate(k)),
+            leo.at[mate(k), pl.ds(half * 2, 2)], o_ref.at[slot, pl.ds(half * 2, 2)],
+            sb.at[half, k], rb.at[half, t], owner(k),
         )
 
     def small(k):
@@ -310,14 +353,11 @@
     products(0, range(EARLY, 21))
     sums = contracts(0, (zero, zero))
     products(1, range(EARLY, EARLY + 4))
+    for k in ORDER + (0,):
+        pl.when(jnp.logical_and(goes(k), mate(k) // 2 == 7 * other))(lambda k=k: lengths(k, slot).start())
     for k in ORDER:
-
-        @pl.when(mate(k) // 2 == 7 * other)
-        def _(k=k):
-            lengths(k).start()
-
-    for k in ORDER:
-        big(0, k).start()
+        big(0, k, slot).start()
+    pl.when(mixed)(lambda: big(0, 0, slot).start())
     products(1, range(EARLY + 4, 21))
     num, den = contracts(2, sums)
     row = lax.broadcasted_iota(jnp.int32, (8, 128), 0)
@@ -330,18 +370,19 @@
         across(n).wait_send()
     for n in range(2):
         sideways(n).wait_send()
-    for k in range(1, 16):
-        own(k).wait_send()
-        for f in range(3):
-            theirs(f, k).wait_send()
+    for n in range(4):
+        swap(n).wait_send()
+    each(range(16), lambda k: own(k).wait_send())
+    for f in range(3):
+        each(range(16), lambda k, f=f: theirs(f, k).wait_send())
     for k in range(1, 16):
         small(k).start()
     for k in ORDER[:6]:
-        big(1, k).start()
-    keep_here = pltpu.make_async_copy(leo.at[i], o_ref.at[i], local.at[0])
-    keep_here.start()
-    keep_length = pltpu.make_async_copy(mg.at[i], om_ref.at[i], local.at[1])
-    keep_length.start()
+        big(1, k, slot).start()
+    keep_here = pltpu.make_async_copy(leo.at[i], o_ref.at[slot], local.at[0])
+    alone(keep_here.start)
+    keep_length = pltpu.make_async_copy(mg.at[i], om_ref.at[slot], local.at[1])
+    alone(keep_length.start)
     for k in range(1, 16):
         small(k).wait_recv()
     total = a1[0]
@@ -354,21 +395,32 @@
     for k in range(1, 16):
         second(k).start()
     for k in ORDER[6:]:
-        big(1, k).start()
+        big(1, k, slot).start()
+    pl.when(mixed)(lambda: big(1, 0, slot).start())
     for k in range(1, 16):
         second(k).wait_recv()
     total = a2[0]
     for q in range(1, 16):
         total = total + a2[q]
     tot_ref[...] = total
-    keep_here.wait()
-    keep_length.wait()
+    alone(keep_here.wait)
+    alone(keep_length.wait)
     for k in range(1, 16):
         second(k).wait_send()
-        lengths(k).wait()
+        lengths(k).wait_send()
+        for half in range(2):
+            big(half, k).wait_send()
+    pl.when(mixed)(lambda: lengths(0).wait_send())
     for half in range(2):
-        for k in range(1, 16):
-            big(half, k).wait()
+        pl.when(mixed)(lambda half=half: big(half, 0).wait_send())
+
+    def arrive(t):
+        lengths(0, t).wait_recv()
+        for half in range(2):
+            big(half, 0, t).wait_recv()
+
+    for t in range(16):
+        pl.when(jnp.logical_or(mixed, slot != t))(functools.partial(arrive, t))
 
 
 def to_planes(tot_ref, pb_ref, o_ref, om_ref, leo_ref, visc_ref, coef_ref, mix):
@@ -452,6 +504,8 @@
             DMA((3, 16)),
             DMA((2,)),
             DMA((2,)),
+            DMA((4,)),
+            DMA((4,)),
             DMA((16,)),
             DMA((16,)),
             DMA((16,)),

time: 95.1 us -> 95.4 us (level)
  no operation moved by 1% of the time
where the time goes in v8:
time: 95.4 us; the launch traced here: 94.8 us
  Pallas kernels  94.2 us (99%)
    pallas_call x1, Pallas kernels, local_step(): pl.pallas_call(core, out_shape=(jax.ShapeDtypeStruct((16, 4, 6, 8, 128),...  89.4 us
    pallas_call x1, Pallas kernels, local_step(): pl.pallas_call(to_planes, out_shape=(jax.ShapeDtypeStruct((6, 8, 64, 128)...  4.79 us

profile of v8, /device:TPU:32, one launch (start us, length us, event | category | flops | bytes accessed | tf_op | source)
XLA Modules:
  0.0 94.8 jit_solution(12247094788513932425)
XLA Ops:
  0.6 89.4 %core.1 = (f32[16,4,6,8,128]{4,3,2,1,0:T(8,128)}, f32[16,4,8,128]{3,2,1,0:T(8,128)}, f32[8,128]{1,0:T(8,128)}) custom-call(f32[3,8,64,128]{3,2,1,0:T(8,128)} %vel_ref.1, f32[256,256]{1,0:T(8,128)} %inv_ref.1, s32[1,256]{1,0:T(1,128)} %bitcast.9, s32[1,256]{1,0:T(1,128)} %bitcast.7), custom_call_target="tpu_custom_call" | custom-call | tf_op jit(solution)/shard_map/core/pallas_call | solution.py:471
  90.1 4.8 %to_planes.1 = (f32[6,8,64,128]{3,2,1,0:T(8,128)}, f32[8,64,128]{2,1,0:T(8,128)}, f32[1,256]{1,0:T(1,128)}) custom-call(f32[8,128]{1,0:T(8,128)} %get-tuple-element.9.tot_ref, s32[1,256]{1,0:T(1,128)} %bitcast.8, f32[3072,128]{1,0:T(8,128)} %bitcast.5, f32[512,128]{1,0:T(8,128)} %bitcast.6), custom_call_target="tpu_custom_call" | custom-call | tf_op jit(solution)/shard_map/to_planes/pallas_call | solution.py:527

commit v9 on v8

--- a/solution.py
+++ b/solution.py
@@ -210,7 +210,7 @@
     each(WINDOWS, lambda k: own(k, i).start(), lambda k: window(k)[0] % 15 == 0)
     alone(lambda: here().start())
 
-    def strip(c, slots):
+    def strip(c, slots, t=0, xs=range(4)):
         y0 = pl.multiple_of(c * 16, 16)
         before = pl.multiple_of(jnp.maximum(y0 - 8, 0), 8)
         after = pl.multiple_of(jnp.minimum(y0 + 16, 248), 8)
@@ -226,18 +226,22 @@
             out, mag = fields_of(u, gx, up, down)
             for k in range(21):
                 if SLOT[k] in slots:
-                    g[SLOT[k], gx - 1] = out[k]
+                    g[t, SLOT[k], gx - 1] = out[k]
             if 2 <= gx <= 5 and 20 in slots:
                 keep(c, gx - 2, mag)
+        box(c, slots, t, xs)
+
+    def box(c, slots, t, xs):
+        y0 = pl.multiple_of(c * 16, 16)
         for k in slots:
-            gs = [g[k, t] for t in range(6)]
-            pairs = [gs[t] + gs[t + 1] for t in range(5)]
-            for x in range(4):
+            gs = {n: g[t, k, n] for n in range(xs[0], xs[-1] + 3)}
+            pairs = {n: gs[n] + gs[n + 1] for n in range(xs[0], xs[-1] + 2)}
+            for x in xs:
                 total = pairs[x] + pairs[x + 1]
-                box = (pltpu.roll(total, 2, 1) + pltpu.roll(total, 126, 1)) + (total + total)
-                hi = box.astype(BF16)
+                both = (pltpu.roll(total, 2, 1) + pltpu.roll(total, 126, 1)) + (total + total)
+                hi = both.astype(BF16)
                 bh[k, pl.ds(y0, 16), pl.ds(x * 128, 128)] = hi
-                bl[k, pl.ds(y0, 16), pl.ds(x * 128, 128)] = (box - hi.astype(F32)).astype(BF16)
+                bl[k, pl.ds(y0, 16), pl.ds(x * 128, 128)] = (both - hi.astype(F32)).astype(BF16)
 
     def keep(c, x, mag):
         block = jnp.where(c // 8 == h, 2 * c - 16 * h, 16)
@@ -253,7 +257,11 @@
         return 0
 
     def late_b(t, _):
-        strip(7 * other + t, range(EARLY, 21))
+        strip(7 * other + t, range(EARLY, 21), t, range(2))
+        return 0
+
+    def late_c(t, _):
+        box(7 * other + t, range(EARLY, 21), t, range(2, 4))
         return 0
 
     def products(half, slots):
@@ -289,15 +297,17 @@
     for k in ORDER + (0,):
         pl.when(jnp.logical_and(goes(k), mate(k) // 2 != 7 * other))(lambda k=k: lengths(k, slot).start())
 
+    alone(lambda: there(0).wait())
+    from_all(lambda q: theirs(0, 0, q).wait_recv())
+    swap(1).start()
     across(2).wait_recv()
     each(WINDOWS, lambda k: theirs(2, k, i).start(), lambda k: window(k)[0] <= 8)
+    alone(lambda: there(1).wait())
+    from_all(lambda q: theirs(1, 0, q).wait_recv())
+    swap(2).start()
     across(3).wait_recv()
     each(WINDOWS, lambda k: theirs(2, k, i).start(), lambda k: window(k)[0] > 8)
     alone(lambda: there(2).start())
-    for f in range(2):
-        alone(lambda f=f: there(f).wait())
-        from_all(lambda q, f=f: theirs(f, 0, q).wait_recv())
-        swap(1 + f).start()
     swap(1).wait_recv()
     swap(2).wait_recv()
     lax.fori_loop(0, 9, late_a, 0)
@@ -352,13 +362,14 @@
     zero = jnp.zeros((8, 128), F32)
     products(0, range(EARLY, 21))
     sums = contracts(0, (zero, zero))
-    products(1, range(EARLY, EARLY + 4))
+    lax.fori_loop(0, 1, late_c, 0)
     for k in ORDER + (0,):
         pl.when(jnp.logical_and(goes(k), mate(k) // 2 == 7 * other))(lambda k=k: lengths(k, slot).start())
     for k in ORDER:
         big(0, k, slot).start()
     pl.when(mixed)(lambda: big(0, 0, slot).start())
-    products(1, range(EARLY + 4, 21))
+    lax.fori_loop(1, 9, late_c, 0)
+    products(1, range(EARLY, 21))
     num, den = contracts(2, sums)
     row = lax.broadcasted_iota(jnp.int32, (8, 128), 0)
     num = jnp.sum(num, axis=0, keepdims=True) * 0.25
@@ -484,7 +495,7 @@
             VMEM((2, 48, 128), F32),
             VMEM((3, 128, 128), F32),
             VMEM((8, 3, 256, 128), F32),
-            VMEM((21, 6, 16, 128), F32),
+            VMEM((9, 21, 6, 16, 128), F32),
             VMEM((21, 256, 512), BF16),
             VMEM((21, 256, 512), BF16),
             VMEM((2, 21, 128, 256), F32),

time: 95.4 us -> 95.9 us (level)
  no operation moved by 1% of the time
where the time goes in v9:
time: 95.9 us; the launch traced here: 95.6 us
  Pallas kernels  94.9 us (99%)
    pallas_call x1, Pallas kernels, local_step(): pl.pallas_call(core, out_shape=(jax.ShapeDtypeStruct((16, 4, 6, 8, 128),...  90.2 us
    pallas_call x1, Pallas kernels, local_step(): pl.pallas_call(to_planes, out_shape=(jax.ShapeDtypeStruct((6, 8, 64, 128)...  4.79 us

profile of v9, /device:TPU:32, one launch (start us, length us, event | category | flops | bytes accessed | tf_op | source)
XLA Modules:
  0.0 95.6 jit_solution(13071421124888030168)
XLA Ops:
  0.6 90.2 %core.1 = (f32[16,4,6,8,128]{4,3,2,1,0:T(8,128)}, f32[16,4,8,128]{3,2,1,0:T(8,128)}, f32[8,128]{1,0:T(8,128)}) custom-call(f32[3,8,64,128]{3,2,1,0:T(8,128)} %vel_ref.1, f32[256,256]{1,0:T(8,128)} %inv_ref.1, s32[1,256]{1,0:T(1,128)} %bitcast.9, s32[1,256]{1,0:T(1,128)} %bitcast.7), custom_call_target="tpu_custom_call" | custom-call | tf_op jit(solution)/shard_map/core/pallas_call | solution.py:482
  90.8 4.8 %to_planes.1 = (f32[6,8,64,128]{3,2,1,0:T(8,128)}, f32[8,64,128]{2,1,0:T(8,128)}, f32[1,256]{1,0:T(1,128)}) custom-call(f32[8,128]{1,0:T(8,128)} %get-tuple-element.9.tot_ref, s32[1,256]{1,0:T(1,128)} %bitcast.8, f32[3072,128]{1,0:T(8,128)} %bitcast.5, f32[512,128]{1,0:T(8,128)} %bitcast.6), custom_call_target="tpu_custom_call" | custom-call | tf_op jit(solution)/shard_map/to_planes/pallas_call | solution.py:538

commit v10 on v9

--- a/solution.py
+++ b/solution.py
@@ -291,23 +291,22 @@
     swap(0).start()
     swap(0).wait_recv()
     lax.fori_loop(0, 7, early, 0)
+    alone(lambda: there(0).wait())
+    from_all(lambda q: theirs(0, 0, q).wait_recv())
+    swap(1).start()
+    for k in ORDER + (0,):
+        pl.when(jnp.logical_and(goes(k), mate(k) // 2 != 7 * other))(lambda k=k: lengths(k, slot).start())
     across(1).wait_recv()
     each(WINDOWS, lambda k: theirs(1, k, i).start())
     alone(lambda: there(1).start())
-    for k in ORDER + (0,):
-        pl.when(jnp.logical_and(goes(k), mate(k) // 2 != 7 * other))(lambda k=k: lengths(k, slot).start())
-
-    alone(lambda: there(0).wait())
-    from_all(lambda q: theirs(0, 0, q).wait_recv())
-    swap(1).start()
     across(2).wait_recv()
     each(WINDOWS, lambda k: theirs(2, k, i).start(), lambda k: window(k)[0] <= 8)
+    across(3).wait_recv()
+    each(WINDOWS, lambda k: theirs(2, k, i).start(), lambda k: window(k)[0] > 8)
+    alone(lambda: there(2).start())
     alone(lambda: there(1).wait())
     from_all(lambda q: theirs(1, 0, q).wait_recv())
     swap(2).start()
-    across(3).wait_recv()
-    each(WINDOWS, lambda k: theirs(2, k, i).start(), lambda k: window(k)[0] > 8)
-    alone(lambda: there(2).start())
     swap(1).wait_recv()
     swap(2).wait_recv()
     lax.fori_loop(0, 9, late_a, 0)

time: 95.9 us -> 94 us (0.980); the launches traced: 95.6 us -> 92.2 us
  Pallas kernels: 94.9 us -> 91.6 us
    pallas_call x1, Pallas kernels: 90.2 us -> 86.8 us  [local_step(): pl.pallas_call(core, out_shape=(jax.ShapeDtypeStruct((16, 4, 6, 8, 128),...]
where the time goes in v10:
time: 94 us; the launch traced here: 92.2 us
  Pallas kernels  91.6 us (97%)
    pallas_call x1, Pallas kernels, local_step(): pl.pallas_call(core, out_shape=(jax.ShapeDtypeStruct((16, 4, 6, 8, 128),...  86.8 us
    pallas_call x1, Pallas kernels, local_step(): pl.pallas_call(to_planes, out_shape=(jax.ShapeDtypeStruct((6, 8, 64, 128)...  4.79 us

profile of v10, /device:TPU:32, one launch (start us, length us, event | category | flops | bytes accessed | tf_op | source)
XLA Modules:
  0.0 92.2 jit_solution(16894022123787387856)
XLA Ops:
  0.6 86.8 %core.1 = (f32[16,4,6,8,128]{4,3,2,1,0:T(8,128)}, f32[16,4,8,128]{3,2,1,0:T(8,128)}, f32[8,128]{1,0:T(8,128)}) custom-call(f32[3,8,64,128]{3,2,1,0:T(8,128)} %vel_ref.1, f32[256,256]{1,0:T(8,128)} %inv_ref.1, s32[1,256]{1,0:T(1,128)} %bitcast.9, s32[1,256]{1,0:T(1,128)} %bitcast.7), custom_call_target="tpu_custom_call" | custom-call | tf_op jit(solution)/shard_map/core/pallas_call | solution.py:481
  87.4 4.8 %to_planes.1 = (f32[6,8,64,128]{3,2,1,0:T(8,128)}, f32[8,64,128]{2,1,0:T(8,128)}, f32[1,256]{1,0:T(1,128)}) custom-call(f32[8,128]{1,0:T(8,128)} %get-tuple-element.9.tot_ref, s32[1,256]{1,0:T(1,128)} %bitcast.8, f32[3072,128]{1,0:T(8,128)} %bitcast.5, f32[512,128]{1,0:T(8,128)} %bitcast.6), custom_call_target="tpu_custom_call" | custom-call | tf_op jit(solution)/shard_map/to_planes/pallas_call | solution.py:537

commit v11 on v10

--- a/solution.py
+++ b/solution.py
@@ -210,64 +210,68 @@
     each(WINDOWS, lambda k: own(k, i).start(), lambda k: window(k)[0] % 15 == 0)
     alone(lambda: here().start())
 
-    def strip(c, slots, t=0, xs=range(4)):
+    def fields(c, slots, t, x0, count):
         y0 = pl.multiple_of(c * 16, 16)
         before = pl.multiple_of(jnp.maximum(y0 - 8, 0), 8)
         after = pl.multiple_of(jnp.minimum(y0 + 16, 248), 8)
         first, last = c == 0, c == 15
-        u = [[r[x, f, pl.ds(y0, 16), :] for x in range(8)] for f in range(3)]
-        for gx in range(1, 7):
+        u = [[r[x0 + x, f, pl.ds(y0, 16), :] for x in range(count + 2)] for f in range(3)]
+        for gx in range(1, count + 1):
             up, down = [], []
             for f in range(3):
-                prev = jnp.where(first, 0.0, r[gx, f, pl.ds(before, 8), :])
-                succ = jnp.where(last, 0.0, r[gx, f, pl.ds(after, 8), :])
+                prev = jnp.where(first, 0.0, r[x0 + gx, f, pl.ds(before, 8), :])
+                succ = jnp.where(last, 0.0, r[x0 + gx, f, pl.ds(after, 8), :])
                 down.append(jnp.concatenate([prev[7:], u[f][gx][:15]], axis=0))
                 up.append(jnp.concatenate([u[f][gx][1:], succ[:1]], axis=0))
             out, mag = fields_of(u, gx, up, down)
             for k in range(21):
                 if SLOT[k] in slots:
-                    g[t, SLOT[k], gx - 1] = out[k]
-            if 2 <= gx <= 5 and 20 in slots:
-                keep(c, gx - 2, mag)
-        box(c, slots, t, xs)
-
-    def box(c, slots, t, xs):
+                    g[t, SLOT[k], x0 + gx - 1] = out[k]
+            if 20 in slots:
+                block = jnp.where(c // 8 == h, 2 * c - 16 * h, 16)
+                mg[block, x0 + gx - 1] = mag[:8]
+                mg[block + 1, x0 + gx - 1] = mag[8:]
+
+    def box(c, slots, t, x0, count):
         y0 = pl.multiple_of(c * 16, 16)
         for k in slots:
-            gs = {n: g[t, k, n] for n in range(xs[0], xs[-1] + 3)}
-            pairs = {n: gs[n] + gs[n + 1] for n in range(xs[0], xs[-1] + 2)}
-            for x in xs:
+            gs = [g[t, k, x0 + n] for n in range(count + 2)]
+            pairs = [gs[n] + gs[n + 1] for n in range(count + 1)]
+            for x in range(count):
                 total = pairs[x] + pairs[x + 1]
                 both = (pltpu.roll(total, 2, 1) + pltpu.roll(total, 126, 1)) + (total + total)
                 hi = both.astype(BF16)
-                bh[k, pl.ds(y0, 16), pl.ds(x * 128, 128)] = hi
-                bl[k, pl.ds(y0, 16), pl.ds(x * 128, 128)] = (both - hi.astype(F32)).astype(BF16)
-
-    def keep(c, x, mag):
-        block = jnp.where(c // 8 == h, 2 * c - 16 * h, 16)
-        mg[block, x] = mag[:8]
-        mg[block + 1, x] = mag[8:]
+                at = pl.ds(pl.multiple_of((x0 + x) * 128, 128), 128)
+                bh[k, pl.ds(y0, 16), at] = hi
+                bl[k, pl.ds(y0, 16), at] = (both - hi.astype(F32)).astype(BF16)
 
     def early(t, _):
-        strip(9 * h + t, range(21))
+        fields(9 * h + t, range(21), 0, 0, 6)
+        box(9 * h + t, range(21), 0, 0, 4)
         return 0
 
     def late_a(t, _):
-        strip(7 * other + t, range(EARLY))
+        fields(7 * other + t, range(EARLY), t, 0, 6)
+        box(7 * other + t, range(EARLY), t, 0, 4)
         return 0
 
+    near_pair = core_of
+    far_pair = 1 - core_of
+
     def late_b(t, _):
-        strip(7 * other + t, range(EARLY, 21), t, range(2))
+        fields(7 * other + t, range(EARLY, 21), t, 2 * near_pair, 4)
+        box(7 * other + t, range(EARLY, 21), t, 2 * near_pair, 2)
         return 0
 
     def late_c(t, _):
-        box(7 * other + t, range(EARLY, 21), t, range(2, 4))
+        fields(7 * other + t, range(EARLY, 21), t, 4 * far_pair, 2)
+        box(7 * other + t, range(EARLY, 21), t, 2 * far_pair, 2)
         return 0
 
     def products(half, slots):
         for k in slots:
-            hi = bh[k, :, pl.ds(half * 256, 256)]
-            lo = bl[k, :, pl.ds(half * 256, 256)]
+            at = pl.ds(pl.multiple_of(half * 256, 256), 256)
+            hi, lo = bh[k, :, at], bl[k, :, at]
             both = jnp.dot(ww[...], hi, preferred_element_type=F32)
             rest = jnp.dot(ww[0:128, :], lo, preferred_element_type=F32)
             ff[half, k] = both[:128] + (both[128:] + rest)
@@ -279,7 +283,7 @@
         return True if k else mixed
 
     def lengths(k, t=0):
-        return send(mg.at[mate(k)], om_ref.at[slot], sm.at[k], rm.at[t], owner(k))
+        return send(mg.at[mate(k), pl.ds(1, 4)], om_ref.at[slot], sm.at[k], rm.at[t], owner(k))
 
     across(0).wait_recv()
     across(4).wait_recv()
@@ -315,17 +319,18 @@
     alone(lambda: there(2).wait())
     from_all(lambda q: theirs(2, 0, q).wait_recv())
     swap(3).start()
-    swap(3).wait_recv()
     lax.fori_loop(0, 9, late_b, 0)
 
     lanes = lax.broadcasted_iota(jnp.int32, (8, 128), 1)
 
-    def contracts(x0, sums):
+    def contracts(half, sums):
+        x0 = 2 * half
+
         def contract(c, sums):
             y0 = pl.multiple_of(c * 8, 8)
             lm_sum, mm_sum = 0.0, 0.0
             for x in range(2):
-                f = [ff[x0 // 2, SLOT[k], pl.ds(y0, 8), pl.ds(x * 128, 128)] for k in range(21)]
+                f = [ff[half, SLOT[k], pl.ds(y0, 8), pl.ds(x * 128, 128)] for k in range(21)]
                 a, b, d = f[0], f[1], f[2]
                 t, p, m = f[3:9], f[9:15], f[15:21]
                 uu = [a * a, b * b, d * d, a * b, a * d, b * d]
@@ -346,10 +351,10 @@
 
         return lax.fori_loop(0, 16, contract, sums)
 
-    def big(half, k, t=0):
+    def big(n, k, t=0):
+        pair = pl.ds(2 * (far_pair if n else near_pair), 2)
         return send(
-            leo.at[mate(k), pl.ds(half * 2, 2)], o_ref.at[slot, pl.ds(half * 2, 2)],
-            sb.at[half, k], rb.at[half, t], owner(k),
+            leo.at[mate(k), pair], o_ref.at[slot, pair], sb.at[n, k], rb.at[n, t], owner(k)
         )
 
     def small(k):
@@ -359,17 +364,18 @@
         return send(s1, a2.at[i], ss2.at[k], rs2.at[k], (px, h * 16 + mate(k)))
 
     zero = jnp.zeros((8, 128), F32)
-    products(0, range(EARLY, 21))
-    sums = contracts(0, (zero, zero))
+    products(near_pair, range(EARLY, 21))
+    sums = contracts(near_pair, (zero, zero))
+    swap(3).wait_recv()
     lax.fori_loop(0, 1, late_c, 0)
-    for k in ORDER + (0,):
-        pl.when(jnp.logical_and(goes(k), mate(k) // 2 == 7 * other))(lambda k=k: lengths(k, slot).start())
     for k in ORDER:
         big(0, k, slot).start()
     pl.when(mixed)(lambda: big(0, 0, slot).start())
     lax.fori_loop(1, 9, late_c, 0)
-    products(1, range(EARLY, 21))
-    num, den = contracts(2, sums)
+    products(far_pair, range(EARLY, 21))
+    for k in ORDER + (0,):
+        pl.when(jnp.logical_and(goes(k), mate(k) // 2 == 7 * other))(lambda k=k: lengths(k, slot).start())
+    num, den = contracts(far_pair, sums)
     row = lax.broadcasted_iota(jnp.int32, (8, 128), 0)
     num = jnp.sum(num, axis=0, keepdims=True) * 0.25
     den = jnp.sum(den, axis=0, keepdims=True) * 0.03125
@@ -391,7 +397,7 @@
         big(1, k, slot).start()
     keep_here = pltpu.make_async_copy(leo.at[i], o_ref.at[slot], local.at[0])
     alone(keep_here.start)
-    keep_length = pltpu.make_async_copy(mg.at[i], om_ref.at[slot], local.at[1])
+    keep_length = pltpu.make_async_copy(mg.at[i, pl.ds(1, 4)], om_ref.at[slot], local.at[1])
     alone(keep_length.start)
     for k in range(1, 16):
         small(k).wait_recv()
@@ -501,7 +507,7 @@
             VMEM((256, 256), BF16),
             VMEM((2, 256, 128), jnp.int32),
             VMEM((16, 4, 6, 8, 128), F32),
-            VMEM((18, 4, 8, 128), F32),
+            VMEM((18, 6, 8, 128), F32),
             VMEM((8, 128), F32),
             VMEM((16, 8, 128), F32),
             VMEM((16, 8, 128), F32),

time: 94 us -> 92.5 us (0.984)
  no operation moved by 1% of the time
where the time goes in v11:
time: 92.5 us; the launch traced here: 91.5 us
  Pallas kernels  90.9 us (98%)
    pallas_call x1, Pallas kernels, local_step(): pl.pallas_call(core, out_shape=(jax.ShapeDtypeStruct((16, 4, 6, 8, 128),...  86.1 us
    pallas_call x1, Pallas kernels, local_step(): pl.pallas_call(to_planes, out_shape=(jax.ShapeDtypeStruct((6, 8, 64, 128)...  4.79 us

profile of v11, /device:TPU:32, one launch (start us, length us, event | category | flops | bytes accessed | tf_op | source)
XLA Modules:
  0.0 91.5 jit_solution(10817892264131122940)
XLA Ops:
  0.6 86.1 %core.1 = (f32[16,4,6,8,128]{4,3,2,1,0:T(8,128)}, f32[16,4,8,128]{3,2,1,0:T(8,128)}, f32[8,128]{1,0:T(8,128)}) custom-call(f32[3,8,64,128]{3,2,1,0:T(8,128)} %vel_ref.1, f32[256,256]{1,0:T(8,128)} %inv_ref.1, s32[1,256]{1,0:T(1,128)} %bitcast.9, s32[1,256]{1,0:T(1,128)} %bitcast.7), custom_call_target="tpu_custom_call" | custom-call | tf_op jit(solution)/shard_map/core/pallas_call | solution.py:487
  86.7 4.8 %to_planes.1 = (f32[6,8,64,128]{3,2,1,0:T(8,128)}, f32[8,64,128]{2,1,0:T(8,128)}, f32[1,256]{1,0:T(1,128)}) custom-call(f32[8,128]{1,0:T(8,128)} %get-tuple-element.9.tot_ref, s32[1,256]{1,0:T(1,128)} %bitcast.8, f32[3072,128]{1,0:T(8,128)} %bitcast.5, f32[512,128]{1,0:T(8,128)} %bitcast.6), custom_call_target="tpu_custom_call" | custom-call | tf_op jit(solution)/shard_map/to_planes/pallas_call | solution.py:543

commit v12 on v11

--- a/solution.py
+++ b/solution.py
@@ -15,7 +15,7 @@
 ORDER = (10, 6, 14, 8, 9, 11, 2, 5, 15, 13, 7, 1, 3, 4, 12)
 
 
-WINDOWS = (12, 13, 10, 11, 14, 15, 4, 5, 2, 3, 6, 7, 8, 9, 0, 1)
+WINDOWS = (12, 10, 14, 13, 11, 15, 4, 2, 6, 8, 5, 3, 7, 9, 0, 1)
 
 
 def where_am_i():

time: 92.5 us -> 91.7 us (level)
  no operation moved by 1% of the time
where the time goes in v12:
time: 91.7 us; the launch traced here: 91.3 us
  Pallas kernels  90.7 us (99%)
    pallas_call x1, Pallas kernels, local_step(): pl.pallas_call(core, out_shape=(jax.ShapeDtypeStruct((16, 4, 6, 8, 128),...  85.9 us
    pallas_call x1, Pallas kernels, local_step(): pl.pallas_call(to_planes, out_shape=(jax.ShapeDtypeStruct((6, 8, 64, 128)...  4.79 us

profile of v12, /device:TPU:32, one launch (start us, length us, event | category | flops | bytes accessed | tf_op | source)
XLA Modules:
  0.0 91.3 jit_solution(9537435872795365281)
XLA Ops:
  0.6 85.9 %core.1 = (f32[16,4,6,8,128]{4,3,2,1,0:T(8,128)}, f32[16,4,8,128]{3,2,1,0:T(8,128)}, f32[8,128]{1,0:T(8,128)}) custom-call(f32[3,8,64,128]{3,2,1,0:T(8,128)} %vel_ref.1, f32[256,256]{1,0:T(8,128)} %inv_ref.1, s32[1,256]{1,0:T(1,128)} %bitcast.9, s32[1,256]{1,0:T(1,128)} %bitcast.7), custom_call_target="tpu_custom_call" | custom-call | tf_op jit(solution)/shard_map/core/pallas_call | solution.py:487
  86.6 4.8 %to_planes.1 = (f32[6,8,64,128]{3,2,1,0:T(8,128)}, f32[8,64,128]{2,1,0:T(8,128)}, f32[1,256]{1,0:T(1,128)}) custom-call(f32[8,128]{1,0:T(8,128)} %get-tuple-element.9.tot_ref, s32[1,256]{1,0:T(1,128)} %bitcast.8, f32[3072,128]{1,0:T(8,128)} %bitcast.5, f32[512,128]{1,0:T(8,128)} %bitcast.6), custom_call_target="tpu_custom_call" | custom-call | tf_op jit(solution)/shard_map/to_planes/pallas_call | solution.py:543
